TPU v7x, 32 devices: a 4x4x1 block of a 4x4x8 slice. The times are simulated.
32 devices in a mesh: dp: 1 (over z), gz: 4 (over y), gy: 4 (over x), gx: 2 (over core).
Axes of the slice: x: 4, y: 4, z: 1, core: 2. Of those that a mesh axis runs over, the one named last changes fastest.
The devices are a block of a 4x4x8 slice.
Arguments:
- volume: bfloat16 [32, 96, 192, 192], P('dp', 'gx', 'gy', 'gz')
- cot_out: bfloat16 [32, 96, 192, 192], P('dp', 'gx', 'gy', 'gz')
- filter_taps: float32 [3, 3, 11], replicated
- w_mix: bfloat16 [3, 32, 32], replicated
- b_mix: float32 [3, 32], replicated
Outputs:
- output 1: bfloat16 [32, 96, 192, 192], P('dp', 'gx', 'gy', 'gz')
- output 2: float32 [3, 32, 32], P('dp')
- output 3: float32 [3, 32], P('dp')
All inputs are finite; a program needn't handle non-finite values.
Results may differ from a plain program's by a relative error of at most 0.0144.
Values are sent between devices in bfloat16 or wider.
A program may use at most 768 MiB of HBM per device.

v0:
```python
import jax
import jax.numpy as jnp
from jax import lax
from jax.sharding import PartitionSpec as P

PASS_FORMS = ('cayz,ai->ciyz', 'cxaz,aj->cxjz', 'cxya,ak->cxyk')


def gelu_exact(pre_act):
    return jax.nn.gelu(pre_act, approximate=False)


def band_matrix(taps, width):
    num_taps = taps.shape[0]
    offset = jnp.arange(width + num_taps - 1)[:, None] - jnp.arange(width)[None, :]
    inside = (offset >= 0) & (offset < num_taps)
    picked = taps.astype(jnp.bfloat16)[jnp.clip(offset, 0, num_taps - 1)]
    return jnp.where(inside, picked, jnp.zeros((), jnp.bfloat16))


def band_pass(padded, taps, axis):
    width = padded.shape[axis + 1] - taps.shape[0] + 1
    return jnp.einsum(PASS_FORMS[axis], padded, band_matrix(taps, width), preferred_element_type=jnp.float32)


def with_halo(block, axis_name, axis_size, axis, width):
    array_dim = axis + 1
    length = block.shape[array_dim]
    low_edge = lax.slice_in_dim(block, 0, width, axis=array_dim)
    high_edge = lax.slice_in_dim(block, length - width, length, axis=array_dim)
    if axis_size == 1:
        from_low = jnp.zeros_like(high_edge)
        from_high = jnp.zeros_like(low_edge)
    else:
        to_next = [(rank, rank + 1) for rank in range(axis_size - 1)]
        to_prev = [(rank + 1, rank) for rank in range(axis_size - 1)]
        from_low = lax.ppermute(high_edge, axis_name, to_next)
        from_high = lax.ppermute(low_edge, axis_name, to_prev)
    return jnp.concatenate([from_low, block, from_high], axis=array_dim)


def solution(mesh):
    names = ('gx', 'gy', 'gz')
    sizes = tuple(mesh.shape[axis_name] for axis_name in names)
    vol_spec = P('dp', 'gx', 'gy', 'gz')

    def local_step(volume, cot_out, filter_taps, w_mix, b_mix):
        num_layers = filter_taps.shape[0]
        half = (filter_taps.shape[2] - 1) // 2
        filtered_all = []
        pre_all = []
        vol_cur = volume
        for layer in range(num_layers):
            current = vol_cur
            for axis in range(3):
                padded = with_halo(current, names[axis], sizes[axis], axis, half)
                current = band_pass(padded, filter_taps[layer, axis], axis).astype(jnp.bfloat16)
            pre_act = jnp.einsum('cd,cxyz->dxyz', w_mix[layer], current, preferred_element_type=jnp.float32) + b_mix[layer][:, None, None, None]
            filtered_all.append(current)
            pre_all.append(pre_act)
            if layer + 1 < num_layers:
                vol_cur = (vol_cur.astype(jnp.float32) + gelu_exact(pre_act)).astype(jnp.bfloat16)
        grad_next = cot_out
        grad_w = [None] * num_layers
        grad_b = [None] * num_layers
        for layer in reversed(range(num_layers)):
            _, pullback = jax.vjp(gelu_exact, pre_all[layer])
            scaled = pullback(grad_next.astype(jnp.float32))[0]
            scaled_b = scaled.astype(jnp.bfloat16)
            grad_b[layer] = jnp.sum(scaled, axis=(1, 2, 3))
            grad_w[layer] = jnp.einsum('cxyz,dxyz->cd', filtered_all[layer], scaled_b, preferred_element_type=jnp.float32)
            current = jnp.einsum('cd,dxyz->cxyz', w_mix[layer], scaled_b, preferred_element_type=jnp.float32).astype(jnp.bfloat16)
            for axis in (2, 1, 0):
                padded = with_halo(current, names[axis], sizes[axis], axis, half)
                back = band_pass(padded, filter_taps[layer, axis][::-1], axis)
                current = back.astype(jnp.bfloat16) if axis > 0 else back
            grad_next = (grad_next.astype(jnp.float32) + current).astype(jnp.bfloat16)
        grad_w_sum = lax.psum(jnp.stack(grad_w), names)
        grad_b_sum = lax.psum(jnp.stack(grad_b), names)
        return grad_next, grad_w_sum, grad_b_sum

    return jax.shard_map(local_step, mesh=mesh, in_specs=(vol_spec, vol_spec, P(), P(), P()), out_specs=(vol_spec, P('dp'), P('dp')), check_vma=False)
```

profile of v0, /device:TPU:97, one launch (start us, length us, event | category | flops | bytes accessed | tf_op | source)
XLA Modules:
  0.0 2532.4 jit_solution(8490552451428811807)
XLA Ops:
  70.7 37.9 %convert_bitcast_fusion.11 = bf16[32,48,48,48]{3,1,2,0:T(8,128)(2,1)} fusion(bf16[32,5,48,48]{1,3,2,0:T(8,128)(2,1)} %copy.50, bf16[32,48,48,48]{1,3,2,0:T(8,128)(2,1)} %copy.49, bf16[32,5,48,48]{1,3,2,0:T(8,128)(2,1)} %copy.48, bf16[]{:T(256)} %bitcast.82, bf16[]{:T(256)} %bitcast.83, bf16[]{:T(256)} %bitcast.84, bf16[]{:T(256)} %bitcast.85, ...), kind=kOutput, calls=%fused_computation.184 | convolution fusion | flops 439797312 | bytes 15630358 | tf_op jit(solution)/shard_map/cayz,ai->ciyz/dot_general | solution.py:23
  116.5 38.5 %collective-permute-done.2 = bf16[32,48,5,48]{3,1,2,0:T(8,128)(2,1)S(1)} collective-permute-done((bf16[32,48,5,48]{3,1,2,0:T(8,128)(2,1)S(1)}, bf16[32,48,5,48]{3,1,2,0:T(8,128)(2,1)S(1)}, u32[]{:S(2)}, u32[]{:S(2)}) %collective-permute-start.2) | collective-permute-done | bytes 737312 | tf_op jit(solution)/shard_map/ppermute | solution.py:37
  218.9 37.1 %collective-permute-done.5 = bf16[32,48,48,5]{2,1,3,0:T(8,128)(2,1)S(1)} collective-permute-done((bf16[32,48,48,5]{2,1,3,0:T(8,128)(2,1)S(1)}, bf16[32,48,48,5]{2,1,3,0:T(8,128)(2,1)S(1)}, u32[]{:S(2)}, u32[]{:S(2)}) %collective-permute-start.5) | collective-permute-done | bytes 737312 | tf_op jit(solution)/shard_map/ppermute | solution.py:38
  286.6 98.0 %fusion.30 = (bf16[32,48,48,48]{3,0,2,1:T(8,128)(2,1)S(1)}, f32[32,48,48,48]{3,0,2,1:T(8,128)}, f32[48,48,48,32]{2,3,1,0:T(8,128)}) fusion(bf16[32,48,48,48]{3,2,1,0:T(8,128)(2,1)} %param.5, f32[32]{0:T(128)S(1)} %get-tuple-element.75, bf16[32,48,48,48]{3,2,1,0:T(8,128)(2,1)} %fusion.178, bf16[3,32,32]{2,1,0:T(8,128)(2,1)S(1)} %copy-done.20), kind=kOutput, calls=%fused_computation.56 | convolution fusion | flops 467140608 | bytes 49553920 | tf_op jit(solution)/shard_map/cd,cxyz->dxyz/dot_general | solution.py:58
  422.2 53.7 %convert_bitcast_fusion.9 = bf16[32,48,48,48]{3,1,2,0:T(8,128)(2,1)} fusion(bf16[32,58,48,48]{3,0,2,1:T(8,128)(2,1)} %pad_maximum_fusion.1, bf16[]{:T(256)} %bitcast.135, bf16[]{:T(256)} %bitcast.136, bf16[]{:T(256)} %bitcast.137, bf16[]{:T(256)} %bitcast.138, bf16[]{:T(256)} %bitcast.139, bf16[]{:T(256)} %bitcast.141, bf16[]{:T(256)} %bitcast.140, ...), kind=kOutput, calls=%fused_computation.182 | convolution fusion | flops 414139968 | bytes 15630358 | tf_op jit(solution)/shard_map/cayz,ai->ciyz/dot_general | solution.py:23
  484.1 39.7 %collective-permute-done.8 = bf16[32,48,5,48]{3,1,2,0:T(8,128)(2,1)S(1)} collective-permute-done((bf16[32,48,5,48]{3,1,2,0:T(8,128)(2,1)S(1)}, bf16[32,48,5,48]{3,1,2,0:T(8,128)(2,1)S(1)}, u32[]{:S(2)}, u32[]{:S(2)}) %collective-permute-start.8) | collective-permute-done | bytes 737312 | tf_op jit(solution)/shard_map/ppermute | solution.py:37
  587.1 38.8 %collective-permute-done.11 = bf16[32,48,48,5]{2,1,3,0:T(8,128)(2,1)S(1)} collective-permute-done((bf16[32,48,48,5]{2,1,3,0:T(8,128)(2,1)S(1)}, bf16[32,48,48,5]{2,1,3,0:T(8,128)(2,1)S(1)}, u32[]{:S(2)}, u32[]{:S(2)}) %collective-permute-start.11) | collective-permute-done | bytes 737312 | tf_op jit(solution)/shard_map/ppermute | solution.py:38
  656.7 97.2 %fusion.27 = (bf16[32,48,48,48]{3,0,2,1:T(8,128)(2,1)S(1)}, f32[32,48,48,48]{3,0,2,1:T(8,128)}, f32[48,48,48,32]{2,3,1,0:T(8,128)}) fusion(bf16[32,48,48,48]{3,0,2,1:T(8,128)(2,1)} %copy-done, f32[32]{0:T(128)S(1)} %copy-done.26, bf16[32,48,48,48]{3,2,1,0:T(8,128)(2,1)} %fusion.175, bf16[3,32,32]{2,1,0:T(8,128)(2,1)S(1)} %copy-done.20), kind=kOutput, calls=%fused_computation.48 | convolution fusion | flops 467140608 | bytes 49553920 | tf_op jit(solution)/shard_map/cd,cxyz->dxyz/dot_general | solution.py:58
  790.6 53.7 %convert_bitcast_fusion.7 = bf16[32,48,48,48]{3,1,2,0:T(8,128)(2,1)} fusion(bf16[32,58,48,48]{3,0,2,1:T(8,128)(2,1)} %pad_maximum_fusion.3, bf16[]{:T(256)} %bitcast.52, bf16[]{:T(256)} %bitcast.53, bf16[]{:T(256)} %bitcast.54, bf16[]{:T(256)} %bitcast.55, bf16[]{:T(256)} %bitcast.56, bf16[]{:T(256)} %bitcast.58, bf16[]{:T(256)} %bitcast.57, ...), kind=kOutput, calls=%fused_computation.180 | convolution fusion | flops 414139968 | bytes 15630358 | tf_op jit(solution)/shard_map/cayz,ai->ciyz/dot_general | solution.py:23
  852.2 39.7 %collective-permute-done.14 = bf16[32,48,5,48]{3,1,2,0:T(8,128)(2,1)S(1)} collective-permute-done((bf16[32,48,5,48]{3,1,2,0:T(8,128)(2,1)S(1)}, bf16[32,48,5,48]{3,1,2,0:T(8,128)(2,1)S(1)}, u32[]{:S(2)}, u32[]{:S(2)}) %collective-permute-start.14) | collective-permute-done | bytes 737312 | tf_op jit(solution)/shard_map/ppermute | solution.py:37
  955.1 38.7 %collective-permute-done.17 = bf16[32,48,48,5]{2,1,3,0:T(8,128)(2,1)S(1)} collective-permute-done((bf16[32,48,48,5]{2,1,3,0:T(8,128)(2,1)S(1)}, bf16[32,48,48,5]{2,1,3,0:T(8,128)(2,1)S(1)}, u32[]{:S(2)}, u32[]{:S(2)}) %collective-permute-start.17) | collective-permute-done | bytes 737312 | tf_op jit(solution)/shard_map/ppermute | solution.py:38
  1024.7 106.9 %fusion.1156 = (f32[32]{0:T(128)}, bf16[32,48,48,48]{3,0,2,1:T(8,128)(2,1)}) fusion(bf16[32,48,48,48]{3,2,1,0:T(8,128)(2,1)} %param.6, f32[32]{0:T(128)S(1)} %copy-done.30, bf16[32,48,48,48]{3,2,1,0:T(8,128)(2,1)} %fusion.172, bf16[3,32,32]{2,1,0:T(8,128)(2,1)S(1)} %copy-done.20), kind=kOutput, calls=%fused_computation.977 | convolution fusion | flops 491913184 | bytes 21242496 | tf_op jit(solution)/shard_map/cd,cxyz->dxyz/dot_general | solution.py:58
  1357.2 34.0 %collective-permute-done.21 = bf16[32,48,5,48]{3,1,2,0:T(8,128)(2,1)} collective-permute-done((bf16[32,48,5,48]{3,1,2,0:T(8,128)(2,1)S(1)}, bf16[32,48,5,48]{3,1,2,0:T(8,128)(2,1)}, u32[]{:S(2)}, u32[]{:S(2)}) %collective-permute-start.21) | collective-permute-done | bytes 737312 | tf_op jit(solution)/shard_map/ppermute | solution.py:38
  1465.7 32.4 %fusion.109 = f32[48,32,48,48]{3,0,2,1:T(8,128)} fusion(bf16[32,58,48,48]{3,2,1,0:T(8,128)(2,1)} %pad_maximum_fusion.5, bf16[]{:T(256)} %bitcast.9, bf16[]{:T(256)} %bitcast.10, bf16[]{:T(256)} %bitcast.11, bf16[]{:T(256)} %bitcast.12, bf16[]{:T(256)} %bitcast.13, bf16[]{:T(256)} %bitcast.15, bf16[]{:T(256)} %bitcast.14, bf16[]{:T(256)} %bitcast.2, ...), kind=kOutput, calls=%fused_computation.138 | convolution fusion | flops 410601024 | bytes 22708246 | tf_op jit(solution)/shard_map/cayz,ai->ciyz/dot_general | solution.py:23
  1498.1 67.5 %fusion.1115 = (f32[32]{0:T(128)}, bf16[32,48,48,48]{3,0,2,1:T(8,128)(2,1)}, bf16[32,48,48,48]{3,0,2,1:T(8,128)(2,1)}) fusion(f32[32,48,48,48]{3,0,2,1:T(8,128)} %get-tuple-element.17, f32[48,48,48,32]{2,3,1,0:T(8,128)} %get-tuple-element.276, f32[32]{0:T(128)S(1)} %copy-done.27, f32[48,32,48,48]{3,0,2,1:T(8,128)} %fusion.109, bf16[32,48,48,48]{3,2,1,0:T(8,128)(2,1)} %param.6), kind=kLoop, calls=%fused_computation.940 | loop fusion | flops 70778848 | bytes 63701248 | tf_op jit(solution)/shard_map/reduce_sum | solution.py:70
  1791.9 36.2 %collective-permute-done.27 = bf16[32,48,5,48]{3,1,2,0:T(8,128)(2,1)} collective-permute-done((bf16[32,48,5,48]{3,1,2,0:T(8,128)(2,1)S(1)}, bf16[32,48,5,48]{3,1,2,0:T(8,128)(2,1)}, u32[]{:S(2)}, u32[]{:S(2)}) %collective-permute-start.27) | collective-permute-done | bytes 737312 | tf_op jit(solution)/shard_map/ppermute | solution.py:38
  1901.8 32.4 %fusion.107 = f32[48,32,48,48]{3,0,2,1:T(8,128)} fusion(bf16[32,58,48,48]{3,2,1,0:T(8,128)(2,1)} %pad_maximum_fusion.6, bf16[]{:T(256)} %bitcast.213, bf16[]{:T(256)} %bitcast.214, bf16[]{:T(256)} %bitcast.215, bf16[]{:T(256)} %bitcast.216, bf16[]{:T(256)} %bitcast.217, bf16[]{:T(256)} %bitcast.219, bf16[]{:T(256)} %bitcast.218, bf16[]{:T(256)} %bitcast.209, ...), kind=kOutput, calls=%fused_computation.136 | convolution fusion | flops 410601024 | bytes 22708246 | tf_op jit(solution)/shard_map/cayz,ai->ciyz/dot_general | solution.py:23
  1934.2 54.5 %fusion.1113 = (f32[32]{0:T(128)}, bf16[32,48,48,48]{3,0,2,1:T(8,128)(2,1)}) fusion(f32[32,48,48,48]{3,0,2,1:T(8,128)} %get-tuple-element.19, f32[48,32,48,48]{3,0,2,1:T(8,128)} %fusion.107, bf16[32,48,48,48]{3,0,2,1:T(8,128)(2,1)} %get-tuple-element.15, f32[48,48,48,32]{2,3,1,0:T(8,128)} %get-tuple-element.275, f32[32]{0:T(128)S(1)} %copy-done.25), kind=kLoop, calls=%fused_computation.939 | loop fusion | flops 70778848 | bytes 56623360 | tf_op jit(solution)/shard_map/reduce_sum | solution.py:70
  2080.2 42.8 %fusion.199 = f32[1,32,32]{2,1,0:T(8,128)S(1)} fusion(bf16[32,48,48,48]{3,0,2,1:T(8,128)(2,1)} %get-tuple-element.278, bf16[32,48,48,48]{3,2,1,0:T(8,128)(2,1)} %fusion.172), kind=kOutput, calls=%fused_computation.211 | convolution fusion | flops 226492416 | bytes 14159872 | tf_op jit(solution)/shard_map/cxyz,dxyz->cd/dot_general | solution.py:71
  2232.2 43.0 %fusion.194 = f32[1,32,32]{2,1,0:T(8,128)S(1)} fusion(bf16[32,48,48,48]{3,0,2,1:T(8,128)(2,1)} %get-tuple-element.14, bf16[32,48,48,48]{3,2,1,0:T(8,128)(2,1)} %fusion.175), kind=kOutput, calls=%fused_computation.210 | convolution fusion | flops 226492416 | bytes 14159872 | tf_op jit(solution)/shard_map/cxyz,dxyz->cd/dot_general | solution.py:71
  2320.6 42.7 %fusion.189 = f32[1,32,32]{2,1,0:T(8,128)S(1)} fusion(bf16[32,48,48,48]{3,0,2,1:T(8,128)(2,1)} %get-tuple-element.12, bf16[32,48,48,48]{3,2,1,0:T(8,128)(2,1)} %fusion.178), kind=kOutput, calls=%fused_computation.209 | convolution fusion | flops 226492416 | bytes 14159872 | tf_op jit(solution)/shard_map/cxyz,dxyz->cd/dot_general | solution.py:71
  2363.5 45.5 %all-reduce = (f32[3,32,32]{2,1,0:T(8,128)}, f32[3,32]{1,0:T(4,128)}) all-reduce(f32[3,32,32]{2,1,0:T(8,128)S(1)} %pad_maximum_fusion.11, f32[3,32]{1,0:T(4,128)S(1)} %pad_maximum_fusion.12), channel_id=1, replica_groups=mesh['dp'=1,'gz'=4,'gy'=4,'gx'=2] {'gx','gy','gz'}, use_global_device_ids=true, to_apply=%region_0.1 | all-reduce | flops 3168 | bytes 25344 | tf_op jit(solution)/shard_map/psum | solution.py:78
  2429.5 32.3 %fusion.105 = f32[48,32,48,48]{3,0,2,1:T(8,128)} fusion(bf16[32,58,48,48]{3,2,1,0:T(8,128)(2,1)} %pad_maximum_fusion.7, bf16[]{:T(256)} %bitcast.259, bf16[]{:T(256)} %bitcast.260, bf16[]{:T(256)} %bitcast.261, bf16[]{:T(256)} %bitcast.262, bf16[]{:T(256)} %bitcast.263, bf16[]{:T(256)} %bitcast.265, bf16[]{:T(256)} %bitcast.264, bf16[]{:T(256)} %bitcast.255, ...), kind=kOutput, calls=%fused_computation.134 | convolution fusion | flops 410601024 | bytes 22708246 | tf_op jit(solution)/shard_map/cayz,ai->ciyz/dot_general | solution.py:23
  2461.8 62.7 %fusion.23 = bf16[32,48,48,48]{3,0,2,1:T(8,128)(2,1)S(1)} fusion(f32[48,32,48,48]{3,0,2,1:T(8,128)} %fusion.105, f32[48,32,48,48]{3,0,2,1:T(8,128)} %fusion.107, bf16[32,48,48,48]{3,0,2,1:T(8,128)(2,1)} %get-tuple-element.15), kind=kLoop, calls=%fused_computation.35 | loop fusion | flops 21233664 | bytes 42467328 | tf_op jit(solution)/shard_map/convert_element_type | solution.py:77
  (241 shorter events, 1324.7 us)
Async XLA Ops:
  10.6 45.3 %collective-permute-start = (bf16[32,5,48,48]{3,2,1,0:T(8,128)(2,1)}, bf16[32,5,48,48]{3,2,1,0:T(8,128)(2,1)S(1)}, u32[]{:S(2)}, u32[]{:S(2)}) collective-permute-start(bf16[32,5,48,48]{3,2,1,0:T(8,128)(2,1)} %get-tuple-element.54), channel_id=1, source_target_pairs={{0,1},{2,3},{4,5},{6,7},{8,9},{10,11},{12,13},{14,15},{16,17},{18,... | collective-permute-start | bytes 2211848 | tf_op jit(solution)/shard_map/ppermute | solution.py:37
  114.3 44.9 %collective-permute-start.3 = (bf16[32,48,5,48]{3,1,2,0:T(8,128)(2,1)S(1)}, bf16[32,48,5,48]{3,1,2,0:T(8,128)(2,1)}, u32[]{:S(2)}, u32[]{:S(2)}) collective-permute-start(bf16[32,48,5,48]{3,1,2,0:T(8,128)(2,1)S(1)} %get-tuple-element.53), channel_id=1, source_target_pairs={{2,0},{4,2},{6,4},{3,1},{5,3},{7,5},{10,8},{12,10},{14,12},{11,9},... | collective-permute-start | bytes 2211848 | tf_op jit(solution)/shard_map/ppermute | solution.py:38
  211.2 44.8 %collective-permute-start.5 = (bf16[32,48,48,5]{2,1,3,0:T(8,128)(2,1)S(1)}, bf16[32,48,48,5]{2,1,3,0:T(8,128)(2,1)S(1)}, u32[]{:S(2)}, u32[]{:S(2)}) collective-permute-start(bf16[32,48,48,5]{2,1,3,0:T(8,128)(2,1)S(1)} %copy.53), channel_id=1, source_target_pairs={{8,0},{16,8},{24,16},{9,1},{17,9},{25,17},{10,2},{18,10},{26,18},{... | collective-permute-start | bytes 2211848 | tf_op jit(solution)/shard_map/ppermute | solution.py:38
  212.8 44.4 %collective-permute-start.4 = (bf16[32,48,48,5]{2,1,3,0:T(8,128)(2,1)S(1)}, bf16[32,48,48,5]{2,1,3,0:T(8,128)(2,1)S(1)}, u32[]{:S(2)}, u32[]{:S(2)}) collective-permute-start(bf16[32,48,48,5]{2,1,3,0:T(8,128)(2,1)S(1)} %copy.52), channel_id=1, source_target_pairs={{0,8},{8,16},{16,24},{1,9},{9,17},{17,25},{2,10},{10,18},{18,26},{... | collective-permute-start | bytes 2211848 | tf_op jit(solution)/shard_map/ppermute | solution.py:37
  478.8 45.0 %collective-permute-start.8 = (bf16[32,48,5,48]{3,1,2,0:T(8,128)(2,1)S(1)}, bf16[32,48,5,48]{3,1,2,0:T(8,128)(2,1)S(1)}, u32[]{:S(2)}, u32[]{:S(2)}) collective-permute-start(bf16[32,48,5,48]{3,1,2,0:T(8,128)(2,1)S(1)} %get-tuple-element.46), channel_id=1, source_target_pairs={{0,2},{2,4},{4,6},{1,3},{3,5},{5,7},{8,10},{10,12},{12,14},{9,11},... | collective-permute-start | bytes 2211848 | tf_op jit(solution)/shard_map/ppermute | solution.py:37
  482.1 45.8 %collective-permute-start.9 = (bf16[32,48,5,48]{3,1,2,0:T(8,128)(2,1)S(1)}, bf16[32,48,5,48]{3,1,2,0:T(8,128)(2,1)}, u32[]{:S(2)}, u32[]{:S(2)}) collective-permute-start(bf16[32,48,5,48]{3,1,2,0:T(8,128)(2,1)S(1)} %get-tuple-element.47), channel_id=1, source_target_pairs={{2,0},{4,2},{6,4},{3,1},{5,3},{7,5},{10,8},{12,10},{14,12},{11,9},... | collective-permute-start | bytes 2211848 | tf_op jit(solution)/shard_map/ppermute | solution.py:38
  579.9 46.0 %collective-permute-start.11 = (bf16[32,48,48,5]{2,1,3,0:T(8,128)(2,1)S(1)}, bf16[32,48,48,5]{2,1,3,0:T(8,128)(2,1)S(1)}, u32[]{:S(2)}, u32[]{:S(2)}) collective-permute-start(bf16[32,48,48,5]{2,1,3,0:T(8,128)(2,1)S(1)} %copy.62), channel_id=1, source_target_pairs={{8,0},{16,8},{24,16},{9,1},{17,9},{25,17},{10,2},{18,10},{26,18},{... | collective-permute-start | bytes 2211848 | tf_op jit(solution)/shard_map/ppermute | solution.py:38
  581.5 45.6 %collective-permute-start.10 = (bf16[32,48,48,5]{2,1,3,0:T(8,128)(2,1)S(1)}, bf16[32,48,48,5]{2,1,3,0:T(8,128)(2,1)S(1)}, u32[]{:S(2)}, u32[]{:S(2)}) collective-permute-start(bf16[32,48,48,5]{2,1,3,0:T(8,128)(2,1)S(1)} %copy.61), channel_id=1, source_target_pairs={{0,8},{8,16},{16,24},{1,9},{9,17},{17,25},{2,10},{10,18},{18,26},{... | collective-permute-start | bytes 2211848 | tf_op jit(solution)/shard_map/ppermute | solution.py:37
  847.2 44.7 %collective-permute-start.14 = (bf16[32,48,5,48]{3,1,2,0:T(8,128)(2,1)S(1)}, bf16[32,48,5,48]{3,1,2,0:T(8,128)(2,1)S(1)}, u32[]{:S(2)}, u32[]{:S(2)}) collective-permute-start(bf16[32,48,5,48]{3,1,2,0:T(8,128)(2,1)S(1)} %get-tuple-element.40), channel_id=1, source_target_pairs={{0,2},{2,4},{4,6},{1,3},{3,5},{5,7},{8,10},{10,12},{12,14},{9,11},... | collective-permute-start | bytes 2211848 | tf_op jit(solution)/shard_map/ppermute | solution.py:37
  850.2 45.8 %collective-permute-start.15 = (bf16[32,48,5,48]{3,1,2,0:T(8,128)(2,1)S(1)}, bf16[32,48,5,48]{3,1,2,0:T(8,128)(2,1)}, u32[]{:S(2)}, u32[]{:S(2)}) collective-permute-start(bf16[32,48,5,48]{3,1,2,0:T(8,128)(2,1)S(1)} %get-tuple-element.41), channel_id=1, source_target_pairs={{2,0},{4,2},{6,4},{3,1},{5,3},{7,5},{10,8},{12,10},{14,12},{11,9},... | collective-permute-start | bytes 2211848 | tf_op jit(solution)/shard_map/ppermute | solution.py:38
  947.9 46.0 %collective-permute-start.17 = (bf16[32,48,48,5]{2,1,3,0:T(8,128)(2,1)S(1)}, bf16[32,48,48,5]{2,1,3,0:T(8,128)(2,1)S(1)}, u32[]{:S(2)}, u32[]{:S(2)}) collective-permute-start(bf16[32,48,48,5]{2,1,3,0:T(8,128)(2,1)S(1)} %copy.71), channel_id=1, source_target_pairs={{8,0},{16,8},{24,16},{9,1},{17,9},{25,17},{10,2},{18,10},{26,18},{... | collective-permute-start | bytes 2211848 | tf_op jit(solution)/shard_map/ppermute | solution.py:38
  949.5 45.6 %collective-permute-start.16 = (bf16[32,48,48,5]{2,1,3,0:T(8,128)(2,1)S(1)}, bf16[32,48,48,5]{2,1,3,0:T(8,128)(2,1)S(1)}, u32[]{:S(2)}, u32[]{:S(2)}) collective-permute-start(bf16[32,48,48,5]{2,1,3,0:T(8,128)(2,1)S(1)} %copy.70), channel_id=1, source_target_pairs={{0,8},{8,16},{16,24},{1,9},{9,17},{17,25},{2,10},{10,18},{18,26},{... | collective-permute-start | bytes 2211848 | tf_op jit(solution)/shard_map/ppermute | solution.py:37
  1192.6 44.1 %collective-permute-start.18 = (bf16[32,48,48,5]{2,1,3,0:T(8,128)(2,1)S(1)}, bf16[32,48,48,5]{2,1,3,0:T(8,128)(2,1)}, u32[]{:S(2)}, u32[]{:S(2)}) collective-permute-start(bf16[32,48,48,5]{2,1,3,0:T(8,128)(2,1)S(1)} %copy.78), channel_id=1, source_target_pairs={{0,8},{8,16},{16,24},{1,9},{9,17},{17,25},{2,10},{10,18},{18,26},{... | collective-permute-start | bytes 2211848 | tf_op jit(solution)/shard_map/ppermute | solution.py:37
  1222.3 43.9 %collective-permute-start.19 = (bf16[32,48,48,5]{2,1,3,0:T(8,128)(2,1)}, bf16[32,48,48,5]{2,1,3,0:T(8,128)(2,1)}, u32[]{:S(2)}, u32[]{:S(2)}) collective-permute-start(bf16[32,48,48,5]{2,1,3,0:T(8,128)(2,1)} %copy.79), channel_id=1, source_target_pairs={{8,0},{16,8},{24,16},{9,1},{17,9},{25,17},{10,2},{18,10},{26,18},{... | collective-permute-start | bytes 2211848 | tf_op jit(solution)/shard_map/ppermute | solution.py:38
  1626.9 44.4 %collective-permute-start.24 = (bf16[32,48,48,5]{2,1,3,0:T(8,128)(2,1)S(1)}, bf16[32,48,48,5]{2,1,3,0:T(8,128)(2,1)}, u32[]{:S(2)}, u32[]{:S(2)}) collective-permute-start(bf16[32,48,48,5]{2,1,3,0:T(8,128)(2,1)S(1)} %copy.91), channel_id=1, source_target_pairs={{0,8},{8,16},{16,24},{1,9},{9,17},{17,25},{2,10},{10,18},{18,26},{... | collective-permute-start | bytes 2211848 | tf_op jit(solution)/shard_map/ppermute | solution.py:37
  1654.5 45.8 %collective-permute-start.25 = (bf16[32,48,48,5]{2,1,3,0:T(8,128)(2,1)}, bf16[32,48,48,5]{2,1,3,0:T(8,128)(2,1)}, u32[]{:S(2)}, u32[]{:S(2)}) collective-permute-start(bf16[32,48,48,5]{2,1,3,0:T(8,128)(2,1)} %copy.92), channel_id=1, source_target_pairs={{8,0},{16,8},{24,16},{9,1},{17,9},{25,17},{10,2},{18,10},{26,18},{... | collective-permute-start | bytes 2211848 | tf_op jit(solution)/shard_map/ppermute | solution.py:38
  1782.0 46.1 %collective-permute-start.27 = (bf16[32,48,5,48]{3,1,2,0:T(8,128)(2,1)S(1)}, bf16[32,48,5,48]{3,1,2,0:T(8,128)(2,1)}, u32[]{:S(2)}, u32[]{:S(2)}) collective-permute-start(bf16[32,48,5,48]{3,1,2,0:T(8,128)(2,1)S(1)} %copy.97), channel_id=1, source_target_pairs={{2,0},{4,2},{6,4},{3,1},{5,3},{7,5},{10,8},{12,10},{14,12},{11,9},... | collective-permute-start | bytes 2211848 | tf_op jit(solution)/shard_map/ppermute | solution.py:38
  1784.9 45.6 %collective-permute-start.26 = (bf16[32,48,5,48]{3,1,2,0:T(8,128)(2,1)}, bf16[32,48,5,48]{3,1,2,0:T(8,128)(2,1)}, u32[]{:S(2)}, u32[]{:S(2)}) collective-permute-start(bf16[32,48,5,48]{3,1,2,0:T(8,128)(2,1)} %copy.96), channel_id=1, source_target_pairs={{0,2},{2,4},{4,6},{1,3},{3,5},{5,7},{8,10},{10,12},{12,14},{9,11},... | collective-permute-start | bytes 2211848 | tf_op jit(solution)/shard_map/ppermute | solution.py:37
  2073.5 70.7 %collective-permute-start.31 = (bf16[32,48,48,5]{2,1,3,0:T(8,128)(2,1)S(1)}, bf16[32,48,48,5]{2,1,3,0:T(8,128)(2,1)}, u32[]{:S(2)}, u32[]{:S(2)}) collective-permute-start(bf16[32,48,48,5]{2,1,3,0:T(8,128)(2,1)S(1)} %copy.105), channel_id=1, source_target_pairs={{8,0},{16,8},{24,16},{9,1},{17,9},{25,17},{10,2},{18,10},{26,18},{... | collective-permute-start | bytes 2211848 | tf_op jit(solution)/shard_map/ppermute | solution.py:38
  2074.9 48.2 %collective-permute-start.30 = (bf16[32,48,48,5]{2,1,3,0:T(8,128)(2,1)}, bf16[32,48,48,5]{2,1,3,0:T(8,128)(2,1)}, u32[]{:S(2)}, u32[]{:S(2)}) collective-permute-start(bf16[32,48,48,5]{2,1,3,0:T(8,128)(2,1)} %copy.104), channel_id=1, source_target_pairs={{0,8},{8,16},{16,24},{1,9},{9,17},{17,25},{2,10},{10,18},{18,26},{... | collective-permute-start | bytes 2211848 | tf_op jit(solution)/shard_map/ppermute | solution.py:37
  2225.9 49.3 %collective-permute-start.33 = (bf16[32,48,5,48]{3,1,2,0:T(8,128)(2,1)S(1)}, bf16[32,48,5,48]{3,1,2,0:T(8,128)(2,1)S(1)}, u32[]{:S(2)}, u32[]{:S(2)}) collective-permute-start(bf16[32,48,5,48]{3,1,2,0:T(8,128)(2,1)S(1)} %copy.110), channel_id=1, source_target_pairs={{2,0},{4,2},{6,4},{3,1},{5,3},{7,5},{10,8},{12,10},{14,12},{11,9},... | collective-permute-start | bytes 2211848 | tf_op jit(solution)/shard_map/ppermute | solution.py:38
  2227.2 48.8 %collective-permute-start.32 = (bf16[32,48,5,48]{3,1,2,0:T(8,128)(2,1)S(1)}, bf16[32,48,5,48]{3,1,2,0:T(8,128)(2,1)S(1)}, u32[]{:S(2)}, u32[]{:S(2)}) collective-permute-start(bf16[32,48,5,48]{3,1,2,0:T(8,128)(2,1)S(1)} %copy.109), channel_id=1, source_target_pairs={{0,2},{2,4},{4,6},{1,3},{3,5},{5,7},{8,10},{10,12},{12,14},{9,11},... | collective-permute-start | bytes 2211848 | tf_op jit(solution)/shard_map/ppermute | solution.py:37
  2314.8 94.2 %collective-permute-start.34 = (bf16[32,5,48,48]{3,2,1,0:T(8,128)(2,1)}, bf16[32,5,48,48]{3,2,1,0:T(8,128)(2,1)S(1)}, u32[]{:S(2)}, u32[]{:S(2)}) collective-permute-start(bf16[32,5,48,48]{3,2,1,0:T(8,128)(2,1)} %get-tuple-element.20), channel_id=1, source_target_pairs={{0,1},{2,3},{4,5},{6,7},{8,9},{10,11},{12,13},{14,15},{16,17},{18,... | collective-permute-start | bytes 2211848 | tf_op jit(solution)/shard_map/ppermute | solution.py:37
  2316.1 92.9 %collective-permute-start.35 = (bf16[32,5,48,48]{3,2,1,0:T(8,128)(2,1)}, bf16[32,5,48,48]{3,2,1,0:T(8,128)(2,1)}, u32[]{:S(2)}, u32[]{:S(2)}) collective-permute-start(bf16[32,5,48,48]{3,2,1,0:T(8,128)(2,1)} %get-tuple-element.21), channel_id=1, source_target_pairs={{1,0},{3,2},{5,4},{7,6},{9,8},{11,10},{13,12},{15,14},{17,16},{19,... | collective-permute-start | bytes 2211848 | tf_op jit(solution)/shard_map/ppermute | solution.py:38
  (43 other events, 1791.6 us)
where the time goes:
time: 2550 us; the launch traced here: 2530 us
  matrix products  1060 us (42%)
  local copies, waits for them, and re-layouts  519 us (20%)
  other arithmetic  426 us (17%)
  waiting for transfers between devices  365 us (14%)
  starting transfers between devices  114 us (4%)
  blocking collectives  45.5 us (2%)
    dot_general x18, matrix products, band_pass(): jnp.einsum(PASS_FORMS[axis], padded, band_matrix(taps, width), preferred_...  593 us
    dot_general x3, matrix products, local_step(): jnp.einsum('cd,cxyz->dxyz', w_mix[layer], current, preferred_element_type...  302 us
    concatenate x11, other arithmetic, with_halo(): return jnp.concatenate([from_low, block, from_high], axis=array_dim)  241 us
    ppermute x18, waiting for transfers between devices, with_halo(): from_high = lax.ppermute(low_edge, axis_name, to_prev)  219 us
    slice x27, local copies, waits for them, and re-layouts, with_halo(): high_edge = lax.slice_in_dim(block, length - width, length, axis=array_dim)  202 us
    ppermute x18, waiting for transfers between devices, with_halo(): from_low = lax.ppermute(high_edge, axis_name, to_next)  146 us
    dot_general x3, matrix products, local_step(): jnp.einsum('cxyz,dxyz->cd', filtered_all[layer], scaled_b, preferred_elem...  129 us
    reduce_sum x2, other arithmetic, local_step(): grad_b[layer] = jnp.sum(scaled, axis=(1, 2, 3))  122 us
  transfers between devices with their start and end apart: 36, of which 21 were waited for; matrix products, arithmetic and copies ran while one was open for 12% of the time, Pallas kernels for 0%

commit v1 on v0

v1 whole, which is shorter than its diff:
```python
import functools

import jax
import jax.numpy as jnp
from jax import lax
from jax.experimental import pallas as pl
from jax.experimental.pallas import tpu as pltpu
from jax.sharding import PartitionSpec as P

MESH = pl.DeviceIdType.MESH
TILE = 256
ROWS = 16
INV_SQRT2 = 0.7071067811865476
INV_SQRT_2PI = 0.3989422804014327
F32 = jnp.float32
BF16 = jnp.bfloat16


def banded(taps, index, keep):
    num_taps = taps.shape[1]
    out = jnp.zeros((taps.shape[0],) + index.shape, F32)
    for t in range(num_taps):
        out = jnp.where((index == t) & keep, taps[:, t][:, None, None], out)
    return out.astype(BF16)


def grid2(rows, cols):
    return jnp.arange(rows)[:, None], jnp.arange(cols)[None, :]


def x_matrix(taps, half, chans):
    r, n = grid2(3 * TILE, TILE)
    index = r // chans - TILE // chans - n // chans + half
    return banded(taps, index, r % chans == n % chans)


def y_matrix(taps, half, side):
    group = ROWS - 2 * half
    r, k = grid2(group * ROWS, ROWS * ROWS)
    yi, zi = k // ROWS, k % ROWS
    main = banded(taps, yi - r // ROWS, r % ROWS == zi)
    if side is None:
        return main
    r, k = grid2(2 * ROWS, ROWS * ROWS)
    sub, q = r // ROWS, r % ROWS
    yo = sub * (group // 2) + q // half
    zo = q % half + (0 if side == 0 else ROWS - half)
    extra = banded(taps, yi - yo, (zo == zi) & (q < (group // 2) * half))
    return jnp.concatenate([main, extra], axis=1)


def z_matrix(taps, half, ysub, nz):
    r, k = grid2(ysub * nz, ysub * nz + 2 * ROWS)
    yo, zo = r // nz, r % nz
    is_main = k < ysub * nz
    q = (k - ysub * nz) % ROWS
    low = k < ysub * nz + ROWS
    yi = jnp.where(is_main, k // nz, q // half)
    zi = jnp.where(is_main, k % nz, jnp.where(low, q % half - half, nz + q % half))
    keep = (yi == yo) & (is_main | (q < ysub * half))
    return banded(taps, zi - zo + half, keep)


def pick_matrix(half, ysub, nz):
    r, k = grid2(2 * ROWS, ysub * nz)
    q = r % ROWS
    zo = q % half + jnp.where(r < ROWS, 0, nz - half)
    hit = (k // nz == q // half) & (k % nz == zo) & (q < ysub * half)
    return hit.astype(BF16)


def dims(shape, half):
    ny, nz, lanes = shape
    group = ROWS - 2 * half
    return ny, nz, lanes, lanes // TILE, group, group // 2


def lane_ds(tile):
    return pl.ds(pl.multiple_of(tile * TILE, TILE), TILE)


class Links:
    def __init__(self, sizes):
        self.sizes = sizes
        self.pos = {name: lax.axis_index(name) for name in ('gx', 'gy', 'gz')}

    def barrier(self):
        sem = pltpu.get_barrier_semaphore()
        count = 1
        pl.semaphore_signal(sem, inc=1, device_id={'gx': 1 - self.pos['gx']}, device_id_type=MESH)
        for name in ('gy', 'gz'):
            size = self.sizes[name]
            for step in (1, size - 1):
                pl.semaphore_signal(sem, inc=1, device_id={name: lax.rem(self.pos[name] + step, size)}, device_id_type=MESH)
                count += 1
        pl.semaphore_wait(sem, count)

    def pair(self, name, low_src, high_dst, high_src, low_dst, sems, tile):
        send, recv = sems
        pos, size = self.pos[name], self.sizes[name]
        down = pltpu.make_async_remote_copy(low_src, high_dst, send.at[0, tile], recv.at[0, tile], device_id={name: jnp.maximum(pos - 1, 0)}, device_id_type=MESH)
        up = pltpu.make_async_remote_copy(high_src, low_dst, send.at[1, tile], recv.at[1, tile], device_id={name: jnp.minimum(pos + 1, size - 1)}, device_id_type=MESH)
        return (down, pos > 0), (up, pos < size - 1)

    def start(self, flows):
        for copy, has in flows:
            pl.when(has)(copy.start)

    def wait_recv(self, flows):
        (down, has_low), (up, has_high) = flows
        pl.when(has_high)(down.wait_recv)
        pl.when(has_low)(up.wait_recv)

    def wait_send(self, flows):
        for copy, has in flows:
            pl.when(has)(copy.wait_send)

    def zero_edges(self, name, low_ref, high_ref):
        @pl.when(self.pos[name] == 0)
        def _():
            low_ref[...] = jnp.zeros_like(low_ref)

        @pl.when(self.pos[name] == self.sizes[name] - 1)
        def _():
            high_ref[...] = jnp.zeros_like(high_ref)

    def x_edge(self, ext, sems, lanes):
        send, recv = sems
        me = self.pos['gx']
        src = pl.multiple_of(lanes + me * (TILE - lanes), TILE)
        dst = pl.multiple_of(me * (lanes + TILE), TILE)
        return pltpu.make_async_remote_copy(ext.at[:, :, pl.ds(src, TILE)], ext.at[:, :, pl.ds(dst, TILE)], send, recv, device_id={'gx': 1 - me}, device_id_type=MESH)

    def zero_x(self, ext, lanes):
        start = pl.multiple_of((1 - self.pos['gx']) * 0 + self.pos['gx'] * (lanes + TILE), TILE)
        ny = ext.shape[0]

        @pl.loop(0, ny)
        def _(y):
            ext[y, :, pl.ds(start, TILE)] = jnp.zeros((ext.shape[1], TILE), ext.dtype)


def y_flows(links, buf, half, ny, sems, tile):
    cols = lane_ds(tile)
    return links.pair('gy', buf.at[pl.ds(half, half), :, cols], buf.at[pl.ds(ny + half, half), :, cols], buf.at[pl.ds(ny, half), :, cols], buf.at[pl.ds(0, half), :, cols], sems, tile)


def z_flows(links, zs, zr, sems, tile):
    cols = lane_ds(tile)
    return links.pair('gz', zs.at[0, :, :, cols], zr.at[1, :, :, cols], zs.at[1, :, :, cols], zr.at[0, :, :, cols], sems, tile)


def dot(a, b):
    return jnp.dot(a, b, preferred_element_type=F32)


def x_pass_rows(ext, wx, tile, start, count):
    nz = ext.shape[1]
    block = ext[pl.ds(start, count), :, pl.ds(pl.multiple_of(tile * TILE, TILE), 3 * TILE)]
    return dot(block.reshape(count * nz, 3 * TILE), wx[...])


def fwd_kernel(half, sizes, last, *refs):
    if last:
        (v_hbm, wx, lya, lyb, lz, wd, bias, a3_hbm, vext, a1, a2, a3, zs, zr, in_sem, out_sem, xsend, xrecv, ysend, yrecv, zsend, zrecv) = refs
    else:
        (v_hbm, wx, lya, lyb, lz, wd, bias, a3_hbm, vo_hbm, vext, a1, a2, a3, zs, zr, in_sem, out_sem, xsend, xrecv, ysend, yrecv, zsend, zrecv) = refs
    ny, nz, lanes, tiles, group, ysub = dims(v_hbm.shape, half)
    links = Links(sizes)
    me = links.pos['gx']

    def order(step):
        return step + me * (tiles - 1 - 2 * step)

    def fetch(tile):
        return pltpu.make_async_copy(v_hbm.at[:, :, lane_ds(tile)], vext.at[:, :, lane_ds(tile + 1)], in_sem.at[tile])

    edge = order(tiles - 1)
    fetch(edge).start()
    for step in range(tiles - 1):
        fetch(order(step)).start()
    links.zero_edges('gy', a1.at[pl.ds(0, half)], a1.at[pl.ds(ny + half, half)])
    links.zero_edges('gz', zr.at[0], zr.at[1])
    links.zero_x(vext, lanes)
    links.barrier()
    fetch(edge).wait()
    xcopy = links.x_edge(vext, (xsend, xrecv), lanes)
    xcopy.start()
    fetch(order(0)).wait()

    def x_phase(tile):
        count = 8 if ny % 8 == 0 else ysub
        for y in range(0, ny, count):
            out = x_pass_rows(vext, wx, tile, y, count)
            a1[pl.ds(y + half, count), :, lane_ds(tile)] = out.astype(BF16).reshape(count, nz, TILE)
        links.start(y_flows(links, a1, half, ny, (ysend, yrecv), tile))

    @pl.loop(0, tiles - 1)
    def _(step):
        @pl.when(step < tiles - 2)
        def _():
            fetch(order(step + 1)).wait()
        x_phase(order(step))

    xcopy.wait_recv()
    x_phase(edge)

    @pl.loop(0, tiles)
    def _(step):
        tile = order(step)
        cols = lane_ds(tile)
        links.wait_recv(y_flows(links, a1, half, ny, (ysend, yrecv), tile))
        for g in range(ny // group):
            for zb in range(nz // ROWS):
                side = {0: 0, nz // ROWS - 1: 1}.get(zb)
                mat = lya if side == 0 else lyb
                rhs = a1[pl.ds(g * group, ROWS), pl.ds(zb * ROWS, ROWS), cols].reshape(ROWS * ROWS, TILE)
                lhs = mat[...] if side is not None else mat[pl.ds(0, group * ROWS), :]
                out = dot(lhs, rhs).astype(BF16)
                a2[pl.ds(g * group, group), pl.ds(zb * ROWS, ROWS), cols] = out[: group * ROWS].reshape(group, ROWS, TILE)
                if side is not None:
                    zs[side, pl.ds(2 * g, 2), :, cols] = out[group * ROWS :].reshape(2, ROWS, TILE)
        links.start(z_flows(links, zs, zr, (zsend, zrecv), tile))

    xcopy.wait_send()

    def put_a3(tile):
        return pltpu.make_async_copy(a3.at[:, :, lane_ds(tile)], a3_hbm.at[:, :, lane_ds(tile)], out_sem.at[0, tile])

    def put_v(tile):
        return pltpu.make_async_copy(vext.at[:, :, lane_ds(tile + 1)], vo_hbm.at[:, :, lane_ds(tile)], out_sem.at[1, tile])

    @pl.loop(0, tiles)
    def _(step):
        tile = order(step)
        cols = lane_ds(tile)
        links.wait_recv(z_flows(links, zs, zr, (zsend, zrecv), tile))
        for g in range(ny // ysub):
            main = a2[pl.ds(g * ysub, ysub), :, cols].reshape(ysub * nz, TILE)
            rhs = jnp.concatenate([main, zr[0, g, :, cols], zr[1, g, :, cols]], axis=0)
            out = dot(lz[...], rhs).astype(BF16)
            a3[pl.ds(g * ysub, ysub), :, cols] = out.reshape(ysub, nz, TILE)
            if not last:
                pre = dot(out, wd[...]) + bias[...]
                act = 0.5 * pre * (1.0 + lax.erf(pre * INV_SQRT2))
                vcols = lane_ds(tile + 1)
                old = vext[pl.ds(g * ysub, ysub), :, vcols].astype(F32).reshape(ysub * nz, TILE)
                vext[pl.ds(g * ysub, ysub), :, vcols] = (old + act).astype(BF16).reshape(ysub, nz, TILE)
        put_a3(tile).start()
        if not last:
            put_v(tile).start()

    @pl.loop(0, tiles)
    def _(tile):
        links.wait_send(y_flows(links, a1, half, ny, (ysend, yrecv), tile))
        links.wait_send(z_flows(links, zs, zr, (zsend, zrecv), tile))
        put_a3(tile).wait()
        if not last:
            put_v(tile).wait()


def bwd_kernel(half, sizes, a3_hbm, g_hbm, wx, ly, lz, pick, wd, wt, bias, go_hbm, dw_ref, db_ref, a3, grad, sb, d3, d2, dext, zs, zr, in_sem, out_sem, xsend, xrecv, ysend, yrecv, zsend, zrecv):
    ny, nz, lanes, tiles, group, ysub = dims(g_hbm.shape, half)
    links = Links(sizes)
    me = links.pos['gx']

    def order(step):
        return (tiles - 1 - step) + me * (2 * step - tiles + 1)

    def fetch(tile):
        cols = lane_ds(tile)
        return (pltpu.make_async_copy(a3_hbm.at[:, :, cols], a3.at[:, :, cols], in_sem.at[0, tile]), pltpu.make_async_copy(g_hbm.at[:, :, cols], grad.at[:, :, cols], in_sem.at[1, tile]))

    for step in range(tiles):
        for copy in fetch(order(step)):
            copy.start()
    links.zero_edges('gy', d2.at[pl.ds(0, half)], d2.at[pl.ds(ny + half, half)])
    links.zero_edges('gz', zr.at[0], zr.at[1])
    links.zero_x(dext, lanes)
    dw_ref[...] = jnp.zeros_like(dw_ref)
    db_ref[...] = jnp.zeros_like(db_ref)
    links.barrier()

    @pl.loop(0, tiles)
    def _(step):
        tile = order(step)
        cols = lane_ds(tile)
        for copy in fetch(tile):
            copy.wait()
        for g in range(ny // ysub):
            rows = pl.ds(g * ysub, ysub)
            act = a3[rows, :, cols].reshape(ysub * nz, TILE)
            pre = dot(act, wd[...]) + bias[...]
            cot = grad[rows, :, cols].astype(F32).reshape(ysub * nz, TILE)
            slope = 0.5 + 0.5 * lax.erf(pre * INV_SQRT2) + pre * (INV_SQRT_2PI * jnp.exp(-0.5 * pre * pre))
            scaled = slope * cot
            db_ref[...] += jnp.sum(scaled.reshape(ysub * nz // 8, 8, TILE), axis=0)
            low = scaled.astype(BF16)
            sb[pl.ds(g * ysub * nz, ysub * nz), :] = low
            mixed = dot(low, wt[...]).astype(BF16)
            d3[rows, :, cols] = mixed.reshape(ysub, nz, TILE)
            planes = dot(pick[...], mixed).astype(BF16)
            zs[0, g, :, cols] = planes[:ROWS]
            zs[1, g, :, cols] = planes[ROWS:]
        links.start(z_flows(links, zs, zr, (zsend, zrecv), tile))
        acts = a3[:, :, cols].reshape(ny * nz, TILE)
        dw_ref[...] += lax.dot_general(acts, sb[...], (((0,), (0,)), ((), ())), preferred_element_type=F32)

    @pl.loop(0, tiles)
    def _(step):
        tile = order(step)
        cols = lane_ds(tile)
        links.wait_recv(z_flows(links, zs, zr, (zsend, zrecv), tile))
        for g in range(ny // ysub):
            main = d3[pl.ds(g * ysub, ysub), :, cols].reshape(ysub * nz, TILE)
            rhs = jnp.concatenate([main, zr[0, g, :, cols], zr[1, g, :, cols]], axis=0)
            out = dot(lz[...], rhs).astype(BF16)
            d2[pl.ds(g * ysub + half, ysub), :, cols] = out.reshape(ysub, nz, TILE)
        links.start(y_flows(links, d2, half, ny, (ysend, yrecv), tile))

    xcopy = links.x_edge(dext, (xsend, xrecv), lanes)

    @pl.loop(0, tiles)
    def _(step):
        tile = order(step)
        cols = lane_ds(tile)
        links.wait_recv(y_flows(links, d2, half, ny, (ysend, yrecv), tile))
        for g in range(ny // group):
            for zb in range(nz // ROWS):
                rhs = d2[pl.ds(g * group, ROWS), pl.ds(zb * ROWS, ROWS), cols].reshape(ROWS * ROWS, TILE)
                out = dot(ly[...], rhs).astype(BF16)
                dext[pl.ds(g * group, group), pl.ds(zb * ROWS, ROWS), lane_ds(tile + 1)] = out.reshape(group, ROWS, TILE)
        pl.when(step == 0)(xcopy.start)

    def put(tile):
        return pltpu.make_async_copy(grad.at[:, :, lane_ds(tile)], go_hbm.at[:, :, lane_ds(tile)], out_sem.at[tile])

    def x_phase(tile):
        cols = lane_ds(tile)
        count = 8 if ny % 8 == 0 else ysub
        for y in range(0, ny, count):
            rows = pl.ds(y, count)
            spread = x_pass_rows(dext, wx, tile, y, count)
            old = grad[rows, :, cols].astype(F32).reshape(count * nz, TILE)
            grad[rows, :, cols] = (old + spread).astype(BF16).reshape(count, nz, TILE)
        put(tile).start()

    @pl.loop(0, tiles - 1)
    def _(step):
        x_phase(order(tiles - 1 - step))

    xcopy.wait_recv()
    x_phase(order(0))
    xcopy.wait_send()

    @pl.loop(0, tiles)
    def _(tile):
        links.wait_send(y_flows(links, d2, half, ny, (ysend, yrecv), tile))
        links.wait_send(z_flows(links, zs, zr, (zsend, zrecv), tile))
        put(tile).wait()


def link_sems(tiles):
    dma = pltpu.SemaphoreType.DMA
    return [dma, dma, dma((2, tiles)), dma((2, tiles)), dma((2, tiles)), dma((2, tiles))]


def solution(mesh):
    names = ('gx', 'gy', 'gz')
    sizes = {name: mesh.shape[name] for name in names}
    vol_spec = P('dp', 'gx', 'gy', 'gz')
    any_spec = pl.BlockSpec(memory_space=pl.ANY)
    vmem_spec = pl.BlockSpec(memory_space=pltpu.VMEM)
    dma = pltpu.SemaphoreType.DMA

    def local_step(volume, cot_out, filter_taps, w_mix, b_mix):
        chans, nx, ny, nz = volume.shape
        num_layers, _, num_taps = filter_taps.shape
        half = (num_taps - 1) // 2
        lanes = nx * chans
        tiles = lanes // TILE
        reps = TILE // chans
        group = ROWS - 2 * half
        ysub = group // 2
        params = functools.partial(pltpu.CompilerParams, has_side_effects=True, vmem_limit_bytes=60 * 1024 * 1024)
        block = jax.ShapeDtypeStruct((ny, nz, lanes), BF16)
        back_taps = filter_taps[:, :, ::-1]
        wx_f = x_matrix(filter_taps[:, 0], half, chans)
        wx_b = x_matrix(back_taps[:, 0], half, chans)
        lya = y_matrix(filter_taps[:, 1], half, 0)
        lyb = y_matrix(filter_taps[:, 1], half, 1)
        ly_b = y_matrix(back_taps[:, 1], half, None)
        lz_f = z_matrix(filter_taps[:, 2], half, ysub, nz)
        lz_b = z_matrix(back_taps[:, 2], half, ysub, nz)
        pick = pick_matrix(half, ysub, nz)
        same = jnp.eye(reps, dtype=BF16)
        wd = (same[None, :, None, :, None] * w_mix[:, None, :, None, :]).reshape(num_layers, TILE, TILE)
        wt = jnp.swapaxes(wd, 1, 2)
        bias = jnp.tile(b_mix, (1, reps))[:, None, :]

        def to_dense(a):
            return jnp.transpose(a, (2, 3, 1, 0)).reshape(ny, nz, lanes)

        halo = pltpu.VMEM((2, ny // ysub, ROWS, lanes), BF16)
        full = pltpu.VMEM((ny, nz, lanes), BF16)
        tall = pltpu.VMEM((ny + 2 * half, nz, lanes), BF16)
        wide = pltpu.VMEM((ny, nz, lanes + 2 * TILE), BF16)

        cur = to_dense(volume)
        acts = []
        for layer in range(num_layers):
            last = layer + 1 == num_layers
            outs = pl.pallas_call(
                functools.partial(fwd_kernel, half, sizes, last),
                out_shape=[block] * (1 if last else 2),
                in_specs=[any_spec] + [vmem_spec] * 6,
                out_specs=[any_spec] * (1 if last else 2),
                scratch_shapes=[wide, tall, full, full, halo, halo, dma((tiles,)), dma((2, tiles))] + link_sems(tiles),
                compiler_params=params(collective_id=layer),
                name='fwd_layer',
            )(cur, wx_f[layer], lya[layer], lyb[layer], lz_f[layer], wd[layer], bias[layer])
            acts.append(outs[0])
            if not last:
                cur = outs[1]

        grad = to_dense(cot_out)
        grad_w, grad_b = [None] * num_layers, [None] * num_layers
        for layer in reversed(range(num_layers)):
            grad, dw, db = pl.pallas_call(
                functools.partial(bwd_kernel, half, sizes),
                out_shape=[block, jax.ShapeDtypeStruct((TILE, TILE), F32), jax.ShapeDtypeStruct((8, TILE), F32)],
                in_specs=[any_spec] * 2 + [vmem_spec] * 7,
                out_specs=[any_spec, vmem_spec, vmem_spec],
                scratch_shapes=[full, full, pltpu.VMEM((ny * nz, TILE), BF16), full, tall, wide, halo, halo, dma((2, tiles)), dma((tiles,))] + link_sems(tiles),
                compiler_params=params(collective_id=num_layers + layer),
                name='bwd_layer',
            )(acts[layer], grad, wx_b[layer], ly_b[layer], lz_b[layer], pick, wd[layer], wt[layer], bias[layer])
            dw4 = dw.reshape(reps, chans, reps, chans)
            grad_w[layer] = sum(dw4[i, :, i, :] for i in range(reps))
            grad_b[layer] = jnp.sum(db.reshape(8 * reps, chans), axis=0)
        grad_volume = jnp.transpose(grad.reshape(ny, nz, nx, chans), (3, 2, 0, 1))
        grad_w_sum = lax.psum(jnp.stack(grad_w), names)
        grad_b_sum = lax.psum(jnp.stack(grad_b), names)
        return grad_volume, grad_w_sum, grad_b_sum

    return jax.shard_map(local_step, mesh=mesh, in_specs=(vol_spec, vol_spec, P(), P(), P()), out_specs=(vol_spec, P('dp'), P('dp')), check_vma=False)
```

time: 2550 us -> 582 us (0.23)
  matrix products: 1060 us -> 0 us
  other arithmetic: 426 us -> 9.62 us
  waiting for transfers between devices: 365 us -> 0 us
  local copies, waits for them, and re-layouts: 519 us -> 251 us
  Pallas kernels: 0 us -> 264 us
  starting transfers between devices: 114 us -> 0 us
    dot_general x27 -> x0, matrix products: 1060 us -> none  [the longest x18 593 us: band_pass(): jnp.einsum(PASS_FORMS[axis], padded, band_matrix(taps, width), preferred_...]
    ppermute x36 -> x0, waiting for transfers between devices: 365 us -> none  [the longest x18 219 us: with_halo(): from_high = lax.ppermute(low_edge, axis_name, to_prev)]
    slice x36 -> x15, local copies, waits for them, and re-layouts: 275 us -> 4.54 us  [the longest x6 2.2 us: banded(): out = jnp.where((index == t) & keep, taps[:, t][:, None, None], out)]
    pallas_call x0 -> x6, Pallas kernels: none -> 264 us  [the longest x3 167 us: local_step(): pl.pallas_call(functools.partial(bwd_kernel, half, sizes), out_shape=[blo...]
    concatenate x11 -> x0, other arithmetic: 241 us -> none  [with_halo(): return jnp.concatenate([from_low, block, from_high], axis=array_dim)]
    ppermute x20 -> x0, local copies, waits for them, and re-layouts: 182 us -> none  [the longest x10 95.5 us: with_halo(): from_low = lax.ppermute(high_edge, axis_name, to_next)]
    reduce_sum x2 -> x3, other arithmetic: 122 us -> 0.09 us  [local_step(): grad_b[layer] = jnp.sum(db.reshape(8 * reps, chans), axis=0)]
    ppermute x36 -> x0, starting transfers between devices: 114 us -> none  [the longest x18 62.7 us: with_halo(): from_low = lax.ppermute(high_edge, axis_name, to_next)]
  transfers between devices with their start and end apart: 36 -> 0, of which waited for: 21 -> 0; matrix products, arithmetic and copies ran while one was open for 12% -> 0% of each run, Pallas kernels for 0% -> 0%
where the time goes in v1:
time: 582 us; the launch traced here: 570 us
  Pallas kernels  264 us (45%)
  local copies, waits for them, and re-layouts  251 us (43%)
  blocking collectives  45 us (8%)
  other arithmetic  9.62 us (2%)
    pallas_call x3, Pallas kernels, local_step(): pl.pallas_call(functools.partial(bwd_kernel, half, sizes), out_shape=[blo...  167 us
    pallas_call x3, Pallas kernels, local_step(): pl.pallas_call(functools.partial(fwd_kernel, half, sizes, last), out_shap...  97.1 us
    transpose x2, local copies, waits for them, and re-layouts, to_dense(): return jnp.transpose(a, (2, 3, 1, 0)).reshape(ny, nz, lanes)  84.5 us
    reshape x2, local copies, waits for them, and re-layouts, to_dense(): return jnp.transpose(a, (2, 3, 1, 0)).reshape(ny, nz, lanes)  70.8 us
    unnamed x15, local copies, waits for them, and re-layouts  45.4 us
    psum x1, blocking collectives, local_step(): grad_w_sum = lax.psum(jnp.stack(grad_w), names)  45 us
    reshape x1, local copies, waits for them, and re-layouts, local_step(): grad_volume = jnp.transpose(grad.reshape(ny, nz, nx, chans), (3, 2, 0, 1))  30.6 us

profile of v1, /device:TPU:97, one launch (start us, length us, event | category | flops | bytes accessed | tf_op | source)
XLA Modules:
  0.0 570.3 jit_solution(8694542723795534176)
XLA Ops:
  0.7 0.8 slice_bitcast_fusion.18
  3.5 0.8 fusion.94
  7.5 0.8 copy.40
  18.1 1.1 mul.82
  20.0 2.1 compare_and_fusion.10
  22.2 1.6 select_convert_fusion
  23.7 1.6 select_convert_fusion.1
  25.3 1.1 slice_bitcast_fusion.3
  26.4 1.1 slice_bitcast_fusion
  27.4 42.2 %copy.39 = bf16[48,48,48,32]{3,2,1,0:T(8,128)(2,1)} copy(bf16[48,48,48,32]{1,0,2,3:T(8,128)(2,1)} %bitcast.133) | data formatting | bytes 14155776 | tf_op jit(solution)/shard_map/transpose | solution.py:402
  69.7 35.4 %reshape.859.refs_0_ = bf16[48,48,1536]{2,1,0:T(8,128)(2,1)} reshape(bf16[48,48,48,32]{3,2,1,0:T(8,128)(2,1)} %copy.39) | data formatting | bytes 14155776 | tf_op jit(solution)/shard_map/reshape | solution.py:402
  105.1 34.4 %fwd_layer.3 = (bf16[48,48,1536]{2,1,0:T(8,128)(2,1)}, bf16[48,48,1536]{2,1,0:T(8,128)(2,1)}) custom-call(bf16[48,48,1536]{2,1,0:T(8,128)(2,1)} %reshape.859.refs_0_, bf16[768,256]{1,0:T(8,128)(2,1)} %get-tuple-element.108.refs_1_, bf16[128,256]{1,0:T(8,128)(2,1)} %get-tuple-element.152.refs_2_, bf16[128,256]{1,0:T(8,128)(2,1)} %get-tuple-element.143.refs_3_, ...), custom_call_target="tpu_custom_call" | custom-call | tf_op jit(solution)/shard_map/fwd_layer/pallas_call | solution.py:413
  139.5 32.3 %fwd_layer.4 = (bf16[48,48,1536]{2,1,0:T(8,128)(2,1)}, bf16[48,48,1536]{2,1,0:T(8,128)(2,1)}) custom-call(bf16[48,48,1536]{2,1,0:T(8,128)(2,1)} %get-tuple-element.17.refs_0_, bf16[768,256]{1,0:T(8,128)(2,1)} %get-tuple-element.107.refs_1_, bf16[128,256]{1,0:T(8,128)(2,1)} %get-tuple-element.151.refs_2_, bf16[128,256]{1,0:T(8,128)(2,1)} %get-tuple-element.144.refs_3_, ...), custom_call_target="tpu_custom_call" | custom-call | tf_op jit(solution)/shard_map/fwd_layer/pallas_call | solution.py:413
  171.8 30.4 %fwd_layer.5.a3_hbm = bf16[48,48,1536]{2,1,0:T(8,128)(2,1)} custom-call(bf16[48,48,1536]{2,1,0:T(8,128)(2,1)} %get-tuple-element.19.refs_0_, bf16[768,256]{1,0:T(8,128)(2,1)} %get-tuple-element.106.refs_1_, bf16[128,256]{1,0:T(8,128)(2,1)} %get-tuple-element.153.refs_2_, bf16[128,256]{1,0:T(8,128)(2,1)} %get-tuple-element.142.refs_3_, ...), custom_call_target="tpu_custom_call" | custom-call | tf_op jit(solution)/shard_map/fwd_layer/pallas_call | solution.py:413
  202.2 42.2 %copy.44 = bf16[48,48,48,32]{3,2,1,0:T(8,128)(2,1)} copy(bf16[48,48,48,32]{1,0,2,3:T(8,128)(2,1)} %bitcast.134) | data formatting | bytes 14155776 | tf_op jit(solution)/shard_map/transpose | solution.py:402
  244.5 35.4 %reshape.860.g_hbm = bf16[48,48,1536]{2,1,0:T(8,128)(2,1)} reshape(bf16[48,48,48,32]{3,2,1,0:T(8,128)(2,1)} %copy.44) | data formatting | bytes 14155776 | tf_op jit(solution)/shard_map/reshape | solution.py:402
  279.9 54.7 %bwd_layer.3 = (bf16[48,48,1536]{2,1,0:T(8,128)(2,1)}, f32[256,256]{1,0:T(8,128)}, f32[8,256]{1,0:T(8,128)}) custom-call(bf16[48,48,1536]{2,1,0:T(8,128)(2,1)} %fwd_layer.5.a3_hbm, bf16[48,48,1536]{2,1,0:T(8,128)(2,1)} %reshape.860.g_hbm, bf16[768,256]{1,0:T(8,128)(2,1)} %get-tuple-element.105.wx, bf16[96,256]{1,0:T(8,128)(2,1)} %get-tuple-element.150.ly, ...), custom_call_target="tpu_custom_call" | custom-call | tf_op jit(solution)/shard_map/bwd_layer/pallas_call | solution.py:429
  334.6 56.7 %bwd_layer.4 = (bf16[48,48,1536]{2,1,0:T(8,128)(2,1)}, f32[256,256]{1,0:T(8,128)}, f32[8,256]{1,0:T(8,128)}) custom-call(bf16[48,48,1536]{2,1,0:T(8,128)(2,1)} %get-tuple-element.18.a3_hbm, bf16[48,48,1536]{2,1,0:T(8,128)(2,1)} %get-tuple-element.20.g_hbm, bf16[768,256]{1,0:T(8,128)(2,1)} %get-tuple-element.104.wx, bf16[96,256]{1,0:T(8,128)(2,1)} %get-tuple-element.149.ly, ...), custom_call_target="tpu_custom_call" | custom-call | tf_op jit(solution)/shard_map/bwd_layer/pallas_call | solution.py:429
  391.4 55.3 %bwd_layer.5 = (bf16[48,48,1536]{2,1,0:T(8,128)(2,1)}, f32[256,256]{1,0:T(8,128)}, f32[8,256]{1,0:T(8,128)}) custom-call(bf16[48,48,1536]{2,1,0:T(8,128)(2,1)} %get-tuple-element.16.a3_hbm, bf16[48,48,1536]{2,1,0:T(8,128)(2,1)} %get-tuple-element.21.g_hbm, bf16[768,256]{1,0:T(8,128)(2,1)} %get-tuple-element.103.wx, bf16[96,256]{1,0:T(8,128)(2,1)} %get-tuple-element.148.ly, ...), custom_call_target="tpu_custom_call" | custom-call | tf_op jit(solution)/shard_map/bwd_layer/pallas_call | solution.py:429
  446.7 0.8 reshape.865
  447.8 1.2 reshape.862
  450.4 45.0 %all-reduce = (f32[3,32,32]{2,1,0:T(8,128)}, f32[3,32]{1,0:T(4,128)}) all-reduce(f32[3,32,32]{2,1,0:T(8,128)S(1)} %pad_maximum_fusion.2, f32[3,32]{1,0:T(4,128)S(1)} %pad_maximum_fusion.3), channel_id=1, replica_groups=mesh['dp'=1,'gz'=4,'gy'=4,'gx'=2] {'gx','gy','gz'}, use_global_device_ids=true, to_apply=%region_0.1 | all-reduce | flops 3168 | bytes 25344 | tf_op jit(solution)/shard_map/psum | solution.py:442
  495.4 30.6 %reshape.861 = bf16[48,48,48,32]{3,2,1,0:T(8,128)(2,1)} reshape(bf16[48,48,1536]{2,1,0:T(8,128)(2,1)} %get-tuple-element.22) | data formatting | bytes 14155776 | tf_op jit(solution)/shard_map/reshape | solution.py:441
  525.9 44.2 %copy.69 = bf16[32,48,48,48]{3,2,1,0:T(8,128)(2,1)} copy(bf16[32,48,48,48]{0,1,3,2:T(8,128)(2,1)} %bitcast.132) | data formatting | bytes 14155776
  (82 shorter events, 17.2 us)
Async XLA Ops:
  391.4 56.2 %copy-start.3 = (f32[8,256]{1,0:T(8,128)S(1)}, f32[8,256]{1,0:T(8,128)}, u32[]{:S(2)}) copy-start(f32[8,256]{1,0:T(8,128)} %get-tuple-element.27) | copy-start | bytes 24580
  391.4 56.3 %copy-start.2 = (f32[8,256]{1,0:T(8,128)S(1)}, f32[8,256]{1,0:T(8,128)}, u32[]{:S(2)}) copy-start(f32[8,256]{1,0:T(8,128)} %get-tuple-element.28) | copy-start | bytes 24580
  446.7 2.5 copy-start.1
  449.0 1.0 copy-start

commit v2 on v1

--- a/solution.py
+++ b/solution.py
@@ -2,6 +2,7 @@
 
 import jax
 import jax.numpy as jnp
+import numpy as np
 from jax import lax
 from jax.experimental import pallas as pl
 from jax.experimental.pallas import tpu as pltpu
@@ -10,63 +11,174 @@
 MESH = pl.DeviceIdType.MESH
 TILE = 256
 ROWS = 16
+LANE = 128
+SUB = 8
+VMEM_BYTES = 60 * 1024 * 1024
 INV_SQRT2 = 0.7071067811865476
 INV_SQRT_2PI = 0.3989422804014327
 F32 = jnp.float32
 BF16 = jnp.bfloat16
 
 
-def banded(taps, index, keep):
-    num_taps = taps.shape[1]
-    out = jnp.zeros((taps.shape[0],) + index.shape, F32)
-    for t in range(num_taps):
-        out = jnp.where((index == t) & keep, taps[:, t][:, None, None], out)
-    return out.astype(BF16)
+def valid_index(index, keep, num_taps):
+    return np.where(keep & (index >= 0) & (index < num_taps), index, -1).astype(np.int32)
 
 
 def grid2(rows, cols):
-    return jnp.arange(rows)[:, None], jnp.arange(cols)[None, :]
-
-
-def x_matrix(taps, half, chans):
+    return np.arange(rows)[:, None], np.arange(cols)[None, :]
+
+
+def x_index(num_taps, chans):
     r, n = grid2(3 * TILE, TILE)
-    index = r // chans - TILE // chans - n // chans + half
-    return banded(taps, index, r % chans == n % chans)
-
-
-def y_matrix(taps, half, side):
+    index = r // chans - TILE // chans - n // chans + num_taps // 2
+    return valid_index(index, r % chans == n % chans, num_taps)
+
+
+def y_index(num_taps):
+    half = num_taps // 2
     group = ROWS - 2 * half
     r, k = grid2(group * ROWS, ROWS * ROWS)
     yi, zi = k // ROWS, k % ROWS
-    main = banded(taps, yi - r // ROWS, r % ROWS == zi)
-    if side is None:
-        return main
+    parts = [valid_index(yi - r // ROWS, r % ROWS == zi, num_taps)]
     r, k = grid2(2 * ROWS, ROWS * ROWS)
-    sub, q = r // ROWS, r % ROWS
-    yo = sub * (group // 2) + q // half
-    zo = q % half + (0 if side == 0 else ROWS - half)
-    extra = banded(taps, yi - yo, (zo == zi) & (q < (group // 2) * half))
-    return jnp.concatenate([main, extra], axis=1)
-
-
-def z_matrix(taps, half, ysub, nz):
+    q = r % ROWS
+    yo = r // ROWS * (group // 2) + q // half
+    for first in (0, ROWS - half):
+        keep = (q % half + first == zi) & (q < (group // 2) * half)
+        parts.append(valid_index(yi - yo, keep, num_taps))
+    return np.concatenate(parts, axis=0)
+
+
+def z_index(num_taps, ysub, nz):
+    half = num_taps // 2
     r, k = grid2(ysub * nz, ysub * nz + 2 * ROWS)
     yo, zo = r // nz, r % nz
     is_main = k < ysub * nz
     q = (k - ysub * nz) % ROWS
     low = k < ysub * nz + ROWS
-    yi = jnp.where(is_main, k // nz, q // half)
-    zi = jnp.where(is_main, k % nz, jnp.where(low, q % half - half, nz + q % half))
+    yi = np.where(is_main, k // nz, q // half)
+    zi = np.where(is_main, k % nz, np.where(low, q % half - half, nz + q % half))
     keep = (yi == yo) & (is_main | (q < ysub * half))
-    return banded(taps, zi - zo + half, keep)
+    return valid_index(zi - zo + half, keep, num_taps)
 
 
 def pick_matrix(half, ysub, nz):
     r, k = grid2(2 * ROWS, ysub * nz)
     q = r % ROWS
-    zo = q % half + jnp.where(r < ROWS, 0, nz - half)
+    zo = q % half + np.where(r < ROWS, 0, nz - half)
     hit = (k // nz == q // half) & (k % nz == zo) & (q < ysub * half)
-    return hit.astype(BF16)
+    return jnp.asarray(hit, BF16)
+
+
+def band_kernel(taps, wmix, spread, same, xi, yi, zi, xf, xb, yf, yb, zf, zb, wd, wt):
+    layers, _, num_taps = taps.shape
+    reps = TILE // spread.shape[0]
+    for axis, index, fwd, bwd in ((0, xi, xf, xb), (1, yi, yf, yb), (2, zi, zf, zb)):
+        @pl.loop(0, index.shape[0] // ROWS)
+        def _(chunk):
+            rows = pl.ds(pl.multiple_of(chunk * ROWS, ROWS), ROWS)
+            which = index[rows, :]
+            zero = jnp.zeros(which.shape, F32)
+            out = [[zero] * layers, [zero] * layers]
+            for t in range(num_taps):
+                hit = which == t
+                for layer in range(layers):
+                    out[0][layer] = jnp.where(hit, taps[layer, axis, t], out[0][layer])
+                    out[1][layer] = jnp.where(hit, taps[layer, axis, num_taps - 1 - t], out[1][layer])
+            for layer in range(layers):
+                fwd[layer, rows, :] = out[0][layer].astype(BF16)
+                bwd[layer, rows, :] = out[1][layer].astype(BF16)
+    for layer in range(layers):
+        for dst, axis in ((wd, 1), (wt, 0)):
+            wide = lax.dot_general(wmix[layer], spread[...], (((axis,), (0,)), ((), ())), preferred_element_type=F32)
+            full = jnp.concatenate([wide] * reps, axis=0)
+            dst[layer] = jnp.where(same[...] != 0, full, 0.0).astype(BF16)
+
+
+def band_weights(filter_taps, w_mix, ysub, nz):
+    layers, _, num_taps = filter_taps.shape
+    chans = w_mix.shape[1]
+    r, n = grid2(TILE, TILE)
+    spread = jnp.asarray(r[:chans] == n % chans, BF16)
+    same = jnp.asarray(r // chans == n // chans, jnp.int32)
+    indices = [x_index(num_taps, chans), y_index(num_taps), z_index(num_taps, ysub, nz)]
+    vmem_spec = pl.BlockSpec(memory_space=pltpu.VMEM)
+    shapes = [i.shape for i in indices for _ in range(2)] + [(TILE, TILE)] * 2
+    return pl.pallas_call(
+        band_kernel,
+        out_shape=[jax.ShapeDtypeStruct((layers,) + shape, BF16) for shape in shapes],
+        in_specs=[pl.BlockSpec(memory_space=pltpu.SMEM)] + [vmem_spec] * 6,
+        out_specs=[vmem_spec] * 8,
+        name='band_weights',
+    )(filter_taps, w_mix, spread, same, *[jnp.asarray(i) for i in indices])
+
+
+def entry_kernel(src, dst, rows):
+    chans, nx, sub, nz = src.shape
+
+    @pl.loop(0, nx)
+    def _(x):
+        part = src[:, x].astype(F32).reshape(chans * sub, nz)
+        rows[pl.ds(pl.multiple_of(x * chans * sub, chans * sub), chans * sub), :] = part
+
+    eye = (lax.broadcasted_iota(jnp.int32, (nz, nz), 0) == lax.broadcasted_iota(jnp.int32, (nz, nz), 1)).astype(BF16)
+
+    @pl.loop(0, nx * chans // TILE)
+    def _(tile):
+        for y in range(sub):
+            block = rows[pl.ds(tile * TILE * sub + y, TILE, stride=sub), :].astype(BF16)
+            out = lax.dot_general(eye, block, (((1,), (1,)), ((), ())), preferred_element_type=F32)
+            dst[y, :, lane_ds(tile)] = out.astype(BF16)
+
+
+def to_dense(a):
+    chans, nx, ny, nz = a.shape
+    lanes = nx * chans
+    return pl.pallas_call(
+        entry_kernel,
+        grid=(ny // SUB,),
+        in_specs=[pl.BlockSpec((chans, nx, SUB, nz), lambda i: (0, 0, i, 0))],
+        out_specs=pl.BlockSpec((SUB, nz, lanes), lambda i: (i, 0, 0)),
+        out_shape=jax.ShapeDtypeStruct((ny, nz, lanes), BF16),
+        scratch_shapes=[pltpu.VMEM((lanes * SUB, nz), F32)],
+        compiler_params=pltpu.CompilerParams(vmem_limit_bytes=VMEM_BYTES),
+        name='to_dense',
+    )(a)
+
+
+def leave_kernel(src, dst, rows):
+    sub, nz, lanes = src.shape
+    chans, nx = dst.shape[:2]
+    eye = (lax.broadcasted_iota(jnp.int32, (TILE, TILE), 0) == lax.broadcasted_iota(jnp.int32, (TILE, TILE), 1)).astype(BF16)
+    pad = jnp.zeros((LANE - nz, TILE), BF16)
+
+    @pl.loop(0, lanes // TILE)
+    def _(tile):
+        for y in range(0, sub, 2):
+            block = jnp.concatenate([src[y, :, lane_ds(tile)], pad, src[y + 1, :, lane_ds(tile)], pad], axis=0)
+            out = lax.dot_general(eye, block, (((1,), (1,)), ((), ())), preferred_element_type=F32)
+            rows[pl.ds(tile * TILE * sub + y, TILE, stride=sub), :] = out[:, :LANE]
+            rows[pl.ds(tile * TILE * sub + y + 1, TILE, stride=sub), :] = out[:, LANE:]
+
+    @pl.loop(0, nx)
+    def _(x):
+        part = rows[pl.ds(pl.multiple_of(x * chans * sub, chans * sub), chans * sub), :]
+        dst[:, x] = part[:, :nz].astype(BF16).reshape(chans, sub, nz)
+
+
+def from_dense(a, chans):
+    ny, nz, lanes = a.shape
+    nx = lanes // chans
+    return pl.pallas_call(
+        leave_kernel,
+        grid=(ny // SUB,),
+        in_specs=[pl.BlockSpec((SUB, nz, lanes), lambda i: (i, 0, 0))],
+        out_specs=pl.BlockSpec((chans, nx, SUB, nz), lambda i: (0, 0, i, 0)),
+        out_shape=jax.ShapeDtypeStruct((chans, nx, ny, nz), BF16),
+        scratch_shapes=[pltpu.VMEM((lanes * SUB, LANE), F32)],
+        compiler_params=pltpu.CompilerParams(vmem_limit_bytes=VMEM_BYTES),
+        name='from_dense',
+    )(a)
 
 
 def dims(shape, half):
@@ -162,9 +274,9 @@
 
 def fwd_kernel(half, sizes, last, *refs):
     if last:
-        (v_hbm, wx, lya, lyb, lz, wd, bias, a3_hbm, vext, a1, a2, a3, zs, zr, in_sem, out_sem, xsend, xrecv, ysend, yrecv, zsend, zrecv) = refs
+        (v_hbm, wx, ly, lz, wd, bias, a3_hbm, vext, a1, a2, a3, zs, zr, in_sem, out_sem, xsend, xrecv, ysend, yrecv, zsend, zrecv) = refs
     else:
-        (v_hbm, wx, lya, lyb, lz, wd, bias, a3_hbm, vo_hbm, vext, a1, a2, a3, zs, zr, in_sem, out_sem, xsend, xrecv, ysend, yrecv, zsend, zrecv) = refs
+        (v_hbm, wx, ly, lz, wd, bias, a3_hbm, vo_hbm, vext, a1, a2, a3, zs, zr, in_sem, out_sem, xsend, xrecv, ysend, yrecv, zsend, zrecv) = refs
     ny, nz, lanes, tiles, group, ysub = dims(v_hbm.shape, half)
     links = Links(sizes)
     me = links.pos['gx']
@@ -213,9 +325,14 @@
         for g in range(ny // group):
             for zb in range(nz // ROWS):
                 side = {0: 0, nz // ROWS - 1: 1}.get(zb)
-                mat = lya if side == 0 else lyb
                 rhs = a1[pl.ds(g * group, ROWS), pl.ds(zb * ROWS, ROWS), cols].reshape(ROWS * ROWS, TILE)
-                lhs = mat[...] if side is not None else mat[pl.ds(0, group * ROWS), :]
+                main = group * ROWS
+                if side == 0:
+                    lhs = ly[pl.ds(0, main + 2 * ROWS), :]
+                elif side == 1:
+                    lhs = jnp.concatenate([ly[pl.ds(0, main), :], ly[pl.ds(main + 2 * ROWS, 2 * ROWS), :]], axis=0)
+                else:
+                    lhs = ly[pl.ds(0, main), :]
                 out = dot(lhs, rhs).astype(BF16)
                 a2[pl.ds(g * group, group), pl.ds(zb * ROWS, ROWS), cols] = out[: group * ROWS].reshape(group, ROWS, TILE)
                 if side is not None:
@@ -328,7 +445,7 @@
         for g in range(ny // group):
             for zb in range(nz // ROWS):
                 rhs = d2[pl.ds(g * group, ROWS), pl.ds(zb * ROWS, ROWS), cols].reshape(ROWS * ROWS, TILE)
-                out = dot(ly[...], rhs).astype(BF16)
+                out = dot(ly[pl.ds(0, group * ROWS), :], rhs).astype(BF16)
                 dext[pl.ds(g * group, group), pl.ds(zb * ROWS, ROWS), lane_ds(tile + 1)] = out.reshape(group, ROWS, TILE)
         pl.when(step == 0)(xcopy.start)
 
@@ -382,24 +499,11 @@
         reps = TILE // chans
         group = ROWS - 2 * half
         ysub = group // 2
-        params = functools.partial(pltpu.CompilerParams, has_side_effects=True, vmem_limit_bytes=60 * 1024 * 1024)
+        params = functools.partial(pltpu.CompilerParams, has_side_effects=True, vmem_limit_bytes=VMEM_BYTES)
         block = jax.ShapeDtypeStruct((ny, nz, lanes), BF16)
-        back_taps = filter_taps[:, :, ::-1]
-        wx_f = x_matrix(filter_taps[:, 0], half, chans)
-        wx_b = x_matrix(back_taps[:, 0], half, chans)
-        lya = y_matrix(filter_taps[:, 1], half, 0)
-        lyb = y_matrix(filter_taps[:, 1], half, 1)
-        ly_b = y_matrix(back_taps[:, 1], half, None)
-        lz_f = z_matrix(filter_taps[:, 2], half, ysub, nz)
-        lz_b = z_matrix(back_taps[:, 2], half, ysub, nz)
+        wx_f, wx_b, ly_f, ly_b, lz_f, lz_b, wd, wt = band_weights(filter_taps, w_mix, ysub, nz)
         pick = pick_matrix(half, ysub, nz)
-        same = jnp.eye(reps, dtype=BF16)
-        wd = (same[None, :, None, :, None] * w_mix[:, None, :, None, :]).reshape(num_layers, TILE, TILE)
-        wt = jnp.swapaxes(wd, 1, 2)
         bias = jnp.tile(b_mix, (1, reps))[:, None, :]
-
-        def to_dense(a):
-            return jnp.transpose(a, (2, 3, 1, 0)).reshape(ny, nz, lanes)
 
         halo = pltpu.VMEM((2, ny // ysub, ROWS, lanes), BF16)
         full = pltpu.VMEM((ny, nz, lanes), BF16)
@@ -413,12 +517,12 @@
             outs = pl.pallas_call(
                 functools.partial(fwd_kernel, half, sizes, last),
                 out_shape=[block] * (1 if last else 2),
-                in_specs=[any_spec] + [vmem_spec] * 6,
+                in_specs=[any_spec] + [vmem_spec] * 5,
                 out_specs=[any_spec] * (1 if last else 2),
                 scratch_shapes=[wide, tall, full, full, halo, halo, dma((tiles,)), dma((2, tiles))] + link_sems(tiles),
                 compiler_params=params(collective_id=layer),
                 name='fwd_layer',
-            )(cur, wx_f[layer], lya[layer], lyb[layer], lz_f[layer], wd[layer], bias[layer])
+            )(cur, wx_f[layer], ly_f[layer], lz_f[layer], wd[layer], bias[layer])
             acts.append(outs[0])
             if not last:
                 cur = outs[1]
@@ -438,7 +542,7 @@
             dw4 = dw.reshape(reps, chans, reps, chans)
             grad_w[layer] = sum(dw4[i, :, i, :] for i in range(reps))
             grad_b[layer] = jnp.sum(db.reshape(8 * reps, chans), axis=0)
-        grad_volume = jnp.transpose(grad.reshape(ny, nz, nx, chans), (3, 2, 0, 1))
+        grad_volume = from_dense(grad, chans)
         grad_w_sum = lax.psum(jnp.stack(grad_w), names)
         grad_b_sum = lax.psum(jnp.stack(grad_b), names)
         return grad_volume, grad_w_sum, grad_b_sum

time: 582 us -> 392 us (0.67); the launches traced: 570 us -> 391 us
  local copies, waits for them, and re-layouts: 251 us -> 12.3 us
  Pallas kernels: 264 us -> 333 us
  other arithmetic: 9.62 us -> 0.15 us
    reshape x3 -> x0, local copies, waits for them, and re-layouts: 101 us -> none  [the longest x2 70.8 us: to_dense(): return jnp.transpose(a, (2, 3, 1, 0)).reshape(ny, nz, lanes)]
    transpose x2 -> x0, local copies, waits for them, and re-layouts: 84.5 us -> none  [to_dense(): return jnp.transpose(a, (2, 3, 1, 0)).reshape(ny, nz, lanes)]
    pallas_call x0 -> x4, Pallas kernels: none -> 69.4 us  [the longest x2 40.5 us: to_dense(): pl.pallas_call(entry_kernel, grid=(ny // SUB,), in_specs=[pl.BlockSpec((c...]
    unnamed x15 -> x14, local copies, waits for them, and re-layouts: 45.4 us -> 0.03 us
where the time goes in v2:
time: 392 us; the launch traced here: 391 us
  Pallas kernels  333 us (85%)
  blocking collectives  45.1 us (12%)
  local copies, waits for them, and re-layouts  12.3 us (3%)
    pallas_call x3, Pallas kernels, local_step(): pl.pallas_call(functools.partial(bwd_kernel, half, sizes), out_shape=[blo...  166 us
    pallas_call x3, Pallas kernels, local_step(): pl.pallas_call(functools.partial(fwd_kernel, half, sizes, last), out_shap...  97.2 us
    psum x1, blocking collectives, local_step(): grad_w_sum = lax.psum(jnp.stack(grad_w), names)  45.1 us
    pallas_call x2, Pallas kernels, to_dense(): pl.pallas_call(entry_kernel, grid=(ny // SUB,), in_specs=[pl.BlockSpec((c...  40.5 us
    pallas_call x1, Pallas kernels, from_dense(): pl.pallas_call(leave_kernel, grid=(ny // SUB,), in_specs=[pl.BlockSpec((S...  20.7 us
    pallas_call x1, Pallas kernels, band_weights(): pl.pallas_call(band_kernel, out_shape=[jax.ShapeDtypeStruct((layers,) + s...  8.14 us

profile of v2, /device:TPU:97, one launch (start us, length us, event | category | flops | bytes accessed | tf_op | source)
XLA Modules:
  0.0 391.4 jit_solution(17372154496144064779)
XLA Ops:
  0.6 20.2 %to_dense.2.refs_0_ = bf16[48,48,1536]{2,1,0:T(8,128)(2,1)} custom-call(bf16[32,48,48,48]{3,2,1,0:T(8,128)(2,1)} %src.2), custom_call_target="tpu_custom_call" | custom-call | tf_op jit(solution)/shard_map/to_dense/pallas_call | solution.py:137
  20.9 8.1 %band_weights.1 = (bf16[3,768,256]{2,1,0:T(8,128)(2,1)}, bf16[3,768,256]{2,1,0:T(8,128)(2,1)}, bf16[3,160,256]{2,1,0:T(8,128)(2,1)}, bf16[3,160,256]{2,1,0:T(8,1...) custom-call(f32[3,3,11]{2,1,0:T(4,128)} %taps.1, ...), custom_call_target="tpu_custom_call" | custom-call | tf_op jit(solution)/shard_map/band_weights/pallas_call | solution.py:107
  29.0 3.2 slice_bitcast_fusion
  32.2 1.9 slice_bitcast_fusion.12
  34.0 1.8 slice_bitcast_fusion.18
  35.9 2.1 slice_bitcast_fusion.6
  38.0 0.6 tile.17.refs_5_.bias
  38.7 34.4 %fwd_layer.3 = (bf16[48,48,1536]{2,1,0:T(8,128)(2,1)}, bf16[48,48,1536]{2,1,0:T(8,128)(2,1)}) custom-call(bf16[48,48,1536]{2,1,0:T(8,128)(2,1)} %to_dense.2.refs_0_, bf16[768,256]{1,0:T(8,128)(2,1)} %get-tuple-element.98.refs_1_, bf16[160,256]{1,0:T(8,128)(2,1)} %get-tuple-element.104.refs_2_, bf16[144,176]{1,0:T(8,128)(2,1)} %get-tuple-element.107.refs_3_, ...), custom_call_target="tpu_custom_call" | custom-call | tf_op jit(solution)/shard_map/fwd_layer/pallas_call | solution.py:517
  73.0 0.6 tile.19.refs_5_.bias
  73.7 32.0 %fwd_layer.4 = (bf16[48,48,1536]{2,1,0:T(8,128)(2,1)}, bf16[48,48,1536]{2,1,0:T(8,128)(2,1)}) custom-call(bf16[48,48,1536]{2,1,0:T(8,128)(2,1)} %get-tuple-element.29.refs_0_, bf16[768,256]{1,0:T(8,128)(2,1)} %get-tuple-element.99.refs_1_, bf16[160,256]{1,0:T(8,128)(2,1)} %get-tuple-element.105.refs_2_, bf16[144,176]{1,0:T(8,128)(2,1)} %get-tuple-element.108.refs_3_, ...), custom_call_target="tpu_custom_call" | custom-call | tf_op jit(solution)/shard_map/fwd_layer/pallas_call | solution.py:517
  105.7 0.7 tile.21.refs_5_.bias
  106.4 30.8 %fwd_layer.5.a3_hbm = bf16[48,48,1536]{2,1,0:T(8,128)(2,1)} custom-call(bf16[48,48,1536]{2,1,0:T(8,128)(2,1)} %get-tuple-element.31.refs_0_, bf16[768,256]{1,0:T(8,128)(2,1)} %get-tuple-element.100.refs_1_, bf16[160,256]{1,0:T(8,128)(2,1)} %get-tuple-element.106.refs_2_, bf16[144,176]{1,0:T(8,128)(2,1)} %get-tuple-element.109.refs_3_, ...), custom_call_target="tpu_custom_call" | custom-call | tf_op jit(solution)/shard_map/fwd_layer/pallas_call | solution.py:517
  137.2 20.2 %to_dense.3.g_hbm = bf16[48,48,1536]{2,1,0:T(8,128)(2,1)} custom-call(bf16[32,48,48,48]{3,2,1,0:T(8,128)(2,1)} %src.3), custom_call_target="tpu_custom_call" | custom-call | tf_op jit(solution)/shard_map/to_dense/pallas_call | solution.py:137
  157.4 54.3 %bwd_layer.3 = (bf16[48,48,1536]{2,1,0:T(8,128)(2,1)}, f32[256,256]{1,0:T(8,128)}, f32[8,256]{1,0:T(8,128)}) custom-call(bf16[48,48,1536]{2,1,0:T(8,128)(2,1)} %fwd_layer.5.a3_hbm, bf16[48,48,1536]{2,1,0:T(8,128)(2,1)} %to_dense.3.g_hbm, bf16[768,256]{1,0:T(8,128)(2,1)} %get-tuple-element.49.wx, bf16[160,256]{1,0:T(8,128)(2,1)} %get-tuple-element.85.ly, ...), custom_call_target="tpu_custom_call" | custom-call | tf_op jit(solution)/shard_map/bwd_layer/pallas_call | solution.py:533
  211.8 56.7 %bwd_layer.4 = (bf16[48,48,1536]{2,1,0:T(8,128)(2,1)}, f32[256,256]{1,0:T(8,128)}, f32[8,256]{1,0:T(8,128)}) custom-call(bf16[48,48,1536]{2,1,0:T(8,128)(2,1)} %get-tuple-element.30.a3_hbm, bf16[48,48,1536]{2,1,0:T(8,128)(2,1)} %get-tuple-element.36.g_hbm, bf16[768,256]{1,0:T(8,128)(2,1)} %get-tuple-element.48.wx, bf16[160,256]{1,0:T(8,128)(2,1)} %get-tuple-element.84.ly, ...), custom_call_target="tpu_custom_call" | custom-call | tf_op jit(solution)/shard_map/bwd_layer/pallas_call | solution.py:533
  268.5 55.4 %bwd_layer.5 = (bf16[48,48,1536]{2,1,0:T(8,128)(2,1)}, f32[256,256]{1,0:T(8,128)}, f32[8,256]{1,0:T(8,128)}) custom-call(bf16[48,48,1536]{2,1,0:T(8,128)(2,1)} %get-tuple-element.28.a3_hbm, bf16[48,48,1536]{2,1,0:T(8,128)(2,1)} %get-tuple-element.37.g_hbm, bf16[768,256]{1,0:T(8,128)(2,1)} %get-tuple-element.47.wx, bf16[160,256]{1,0:T(8,128)(2,1)} %get-tuple-element.83.ly, ...), custom_call_target="tpu_custom_call" | custom-call | tf_op jit(solution)/shard_map/bwd_layer/pallas_call | solution.py:533
  324.0 20.7 %from_dense.1 = bf16[32,48,48,48]{3,2,1,0:T(8,128)(2,1)} custom-call(bf16[48,48,1536]{2,1,0:T(8,128)(2,1)} %get-tuple-element.38.src), custom_call_target="tpu_custom_call" | custom-call | tf_op jit(solution)/shard_map/from_dense/pallas_call | solution.py:172
  344.7 0.3 reshape.290
  345.0 0.1 fusion.2
  345.1 0.3 reshape.289
  345.4 0.1 fusion.1
  345.5 0.3 reshape.288
  345.8 0.1 fusion
  346.3 45.1 %all-reduce = (f32[3,32,32]{2,1,0:T(8,128)}, f32[3,32]{1,0:T(4,128)}) all-reduce(f32[3,32,32]{2,1,0:T(8,128)S(1)} %pad_maximum_fusion, f32[3,32]{1,0:T(4,128)S(1)} %pad_maximum_fusion.1), channel_id=1, replica_groups=mesh['dp'=1,'gz'=4,'gy'=4,'gx'=2] {'gx','gy','gz'}, use_global_device_ids=true, to_apply=%region_0.0 | all-reduce | flops 3168 | bytes 25344 | tf_op jit(solution)/shard_map/psum | solution.py:546
  (29 shorter events, 0.4 us)
Async XLA Ops:
  20.9 17.1 %copy-start.6 = (f32[3,32]{1,0:T(4,128)S(1)}, f32[3,32]{1,0:T(4,128)}, u32[]{:S(2)}) copy-start(f32[3,32]{1,0:T(4,128)} %param.15) | copy-start | bytes 1156
  323.9 20.8 %copy-start.2 = (f32[256,256]{1,0:T(8,128)S(1)}, f32[256,256]{1,0:T(8,128)}, u32[]{:S(2)}) copy-start(f32[256,256]{1,0:T(8,128)} %get-tuple-element.41) | copy-start | bytes 786436
  323.9 21.2 %copy-start.1 = (f32[256,256]{1,0:T(8,128)S(1)}, f32[256,256]{1,0:T(8,128)}, u32[]{:S(2)}) copy-start(f32[256,256]{1,0:T(8,128)} %get-tuple-element.40) | copy-start | bytes 786436
  323.9 21.6 %copy-start = (f32[256,256]{1,0:T(8,128)S(1)}, f32[256,256]{1,0:T(8,128)}, u32[]{:S(2)}) copy-start(f32[256,256]{1,0:T(8,128)} %get-tuple-element.39) | copy-start | bytes 786436
  323.9 22.0 %copy-start.3 = (f32[8,256]{1,0:T(8,128)S(1)}, f32[8,256]{1,0:T(8,128)}, u32[]{:S(2)}) copy-start(f32[8,256]{1,0:T(8,128)} %get-tuple-element.44) | copy-start | bytes 24580
  323.9 22.1 %copy-start.4 = (f32[8,256]{1,0:T(8,128)S(1)}, f32[8,256]{1,0:T(8,128)}, u32[]{:S(2)}) copy-start(f32[8,256]{1,0:T(8,128)} %get-tuple-element.43) | copy-start | bytes 24580
  324.0 22.2 %copy-start.5 = (f32[8,256]{1,0:T(8,128)S(1)}, f32[8,256]{1,0:T(8,128)}, u32[]{:S(2)}) copy-start(f32[8,256]{1,0:T(8,128)} %get-tuple-element.42) | copy-start | bytes 24580

commit v3 on v2

v3 whole, which is shorter than its diff:
```python
import functools

import jax
import jax.numpy as jnp
import numpy as np
from jax import lax
from jax.experimental import pallas as pl
from jax.experimental.pallas import tpu as pltpu
from jax.sharding import PartitionSpec as P

MESH = pl.DeviceIdType.MESH
TILE = 256
ROWS = 16
LANE = 128
SUB = 8
VMEM_BYTES = 60 * 1024 * 1024
INV_SQRT2 = 0.7071067811865476
TWO_INV_SQRT_PI = 1.1283791670955126
F32 = jnp.float32
BF16 = jnp.bfloat16


def valid_index(index, keep, num_taps):
    return np.where(keep & (index >= 0) & (index < num_taps), index, -1).astype(np.int32)


def grid2(rows, cols):
    return np.arange(rows)[:, None], np.arange(cols)[None, :]


def x_index(num_taps, chans):
    r, n = grid2(3 * TILE, TILE)
    index = r // chans - TILE // chans - n // chans + num_taps // 2
    return valid_index(index, r % chans == n % chans, num_taps)


def y_index(num_taps):
    half = num_taps // 2
    group = ROWS - 2 * half
    r, k = grid2(group * ROWS, ROWS * ROWS)
    yi, zi = k // ROWS, k % ROWS
    parts = [valid_index(yi - r // ROWS, r % ROWS == zi, num_taps)]
    r, k = grid2(2 * ROWS, ROWS * ROWS)
    q = r % ROWS
    yo = r // ROWS * (group // 2) + q // half
    for first in (0, ROWS - half):
        keep = (q % half + first == zi) & (q < (group // 2) * half)
        parts.append(valid_index(yi - yo, keep, num_taps))
    return np.concatenate(parts, axis=0)


def z_index(num_taps, ysub, nz):
    half = num_taps // 2
    r, k = grid2(ysub * nz, ysub * nz + 2 * ROWS)
    yo, zo = r // nz, r % nz
    is_main = k < ysub * nz
    q = (k - ysub * nz) % ROWS
    low = k < ysub * nz + ROWS
    yi = np.where(is_main, k // nz, q // half)
    zi = np.where(is_main, k % nz, np.where(low, q % half - half, nz + q % half))
    keep = (yi == yo) & (is_main | (q < ysub * half))
    return valid_index(zi - zo + half, keep, num_taps)


def pick_matrix(half, ysub, nz):
    r, k = grid2(2 * ROWS, ysub * nz)
    q = r % ROWS
    zo = q % half + np.where(r < ROWS, 0, nz - half)
    hit = (k // nz == q // half) & (k % nz == zo) & (q < ysub * half)
    return jnp.asarray(hit, BF16)


def band_kernel(taps, wmix, spread, same, xi, yi, zi, xf, xb, yf, yb, zf, zb, wd, wt):
    layers, _, num_taps = taps.shape
    reps = TILE // spread.shape[0]
    for axis, index, fwd, bwd in ((0, xi, xf, xb), (1, yi, yf, yb), (2, zi, zf, zb)):
        @pl.loop(0, index.shape[0] // ROWS)
        def _(chunk):
            rows = pl.ds(pl.multiple_of(chunk * ROWS, ROWS), ROWS)
            which = index[rows, :]
            zero = jnp.zeros(which.shape, F32)
            out = [[zero] * layers, [zero] * layers]
            for t in range(num_taps):
                hit = which == t
                for layer in range(layers):
                    out[0][layer] = jnp.where(hit, taps[layer, axis, t], out[0][layer])
                    out[1][layer] = jnp.where(hit, taps[layer, axis, num_taps - 1 - t], out[1][layer])
            for layer in range(layers):
                fwd[layer, rows, :] = out[0][layer].astype(BF16)
                bwd[layer, rows, :] = out[1][layer].astype(BF16)
    for layer in range(layers):
        for dst, axis in ((wd, 1), (wt, 0)):
            wide = lax.dot_general(wmix[layer], spread[...], (((axis,), (0,)), ((), ())), preferred_element_type=F32)
            full = jnp.concatenate([wide] * reps, axis=0)
            dst[layer] = jnp.where(same[...] != 0, full, 0.0).astype(BF16)


def band_weights(filter_taps, w_mix, ysub, nz):
    layers, _, num_taps = filter_taps.shape
    chans = w_mix.shape[1]
    r, n = grid2(TILE, TILE)
    spread = jnp.asarray(r[:chans] == n % chans, BF16)
    same = jnp.asarray(r // chans == n // chans, jnp.int32)
    indices = [x_index(num_taps, chans), y_index(num_taps), z_index(num_taps, ysub, nz)]
    vmem_spec = pl.BlockSpec(memory_space=pltpu.VMEM)
    shapes = [i.shape for i in indices for _ in range(2)] + [(TILE, TILE)] * 2
    return pl.pallas_call(
        band_kernel,
        out_shape=[jax.ShapeDtypeStruct((layers,) + shape, BF16) for shape in shapes],
        in_specs=[pl.BlockSpec(memory_space=pltpu.SMEM)] + [vmem_spec] * 6,
        out_specs=[vmem_spec] * 8,
        name='band_weights',
    )(filter_taps, w_mix, spread, same, *[jnp.asarray(i) for i in indices])


def entry_kernel(src, dst, rows):
    chans, nx, sub, nz = src.shape

    @pl.loop(0, nx)
    def _(x):
        part = src[:, x].astype(F32).reshape(chans * sub, nz)
        rows[pl.ds(pl.multiple_of(x * chans * sub, chans * sub), chans * sub), :] = part

    eye = (lax.broadcasted_iota(jnp.int32, (nz, nz), 0) == lax.broadcasted_iota(jnp.int32, (nz, nz), 1)).astype(BF16)

    @pl.loop(0, nx * chans // TILE)
    def _(tile):
        for y in range(sub):
            block = rows[pl.ds(tile * TILE * sub + y, TILE, stride=sub), :].astype(BF16)
            out = lax.dot_general(eye, block, (((1,), (1,)), ((), ())), preferred_element_type=F32)
            dst[y, :, lane_ds(tile)] = out.astype(BF16)


def to_dense(a):
    chans, nx, ny, nz = a.shape
    lanes = nx * chans
    return pl.pallas_call(
        entry_kernel,
        grid=(ny // SUB,),
        in_specs=[pl.BlockSpec((chans, nx, SUB, nz), lambda i: (0, 0, i, 0))],
        out_specs=pl.BlockSpec((SUB, nz, lanes), lambda i: (i, 0, 0)),
        out_shape=jax.ShapeDtypeStruct((ny, nz, lanes), BF16),
        scratch_shapes=[pltpu.VMEM((lanes * SUB, nz), F32)],
        compiler_params=pltpu.CompilerParams(vmem_limit_bytes=VMEM_BYTES),
        name='to_dense',
    )(a)


def leave_kernel(src, dst, rows):
    sub, nz, lanes = src.shape
    chans, nx = dst.shape[:2]
    eye = (lax.broadcasted_iota(jnp.int32, (TILE, TILE), 0) == lax.broadcasted_iota(jnp.int32, (TILE, TILE), 1)).astype(BF16)
    pad = jnp.zeros((LANE - nz, TILE), BF16)

    @pl.loop(0, lanes // TILE)
    def _(tile):
        for y in range(0, sub, 2):
            block = jnp.concatenate([src[y, :, lane_ds(tile)], pad, src[y + 1, :, lane_ds(tile)], pad], axis=0)
            out = lax.dot_general(eye, block, (((1,), (1,)), ((), ())), preferred_element_type=F32)
            rows[pl.ds(tile * TILE * sub + y, TILE, stride=sub), :] = out[:, :LANE]
            rows[pl.ds(tile * TILE * sub + y + 1, TILE, stride=sub), :] = out[:, LANE:]

    @pl.loop(0, nx)
    def _(x):
        part = rows[pl.ds(pl.multiple_of(x * chans * sub, chans * sub), chans * sub), :]
        dst[:, x] = part[:, :nz].astype(BF16).reshape(chans, sub, nz)


def from_dense(a, chans):
    ny, nz, lanes = a.shape
    nx = lanes // chans
    return pl.pallas_call(
        leave_kernel,
        grid=(ny // SUB,),
        in_specs=[pl.BlockSpec((SUB, nz, lanes), lambda i: (i, 0, 0))],
        out_specs=pl.BlockSpec((chans, nx, SUB, nz), lambda i: (0, 0, i, 0)),
        out_shape=jax.ShapeDtypeStruct((chans, nx, ny, nz), BF16),
        scratch_shapes=[pltpu.VMEM((lanes * SUB, LANE), F32)],
        compiler_params=pltpu.CompilerParams(vmem_limit_bytes=VMEM_BYTES),
        name='from_dense',
    )(a)


def dims(shape, half):
    ny, nz, lanes = shape
    group = ROWS - 2 * half
    return ny, nz, lanes, lanes // TILE, group, group // 2


def lane_ds(tile):
    return pl.ds(pl.multiple_of(tile * TILE, TILE), TILE)


class Links:
    def __init__(self, sizes):
        self.sizes = sizes
        self.pos = {name: lax.axis_index(name) for name in ('gx', 'gy', 'gz')}

    def barrier(self):
        sem = pltpu.get_barrier_semaphore()
        count = 0
        for name, size in self.sizes.items():
            for step in range(1, size):
                pl.semaphore_signal(sem, inc=1, device_id={name: lax.rem(self.pos[name] + step, size)}, device_id_type=MESH)
                count += 1
        pl.semaphore_wait(sem, count)

    def pair(self, name, low_src, high_src, dst, sems, slot, tile):
        send, recv = sems
        pos, size = self.pos[name], self.sizes[name]
        down = pltpu.make_async_remote_copy(low_src, dst[1], send.at[0, tile], recv.at[slot, 0, tile], device_id={name: jnp.maximum(pos - 1, 0)}, device_id_type=MESH)
        up = pltpu.make_async_remote_copy(high_src, dst[0], send.at[1, tile], recv.at[slot, 1, tile], device_id={name: jnp.minimum(pos + 1, size - 1)}, device_id_type=MESH)
        return (down, pos > 0), (up, pos < size - 1)

    def start(self, flows):
        for copy, has in flows:
            pl.when(has)(copy.start)

    def wait_recv(self, flows):
        (down, has_low), (up, has_high) = flows
        pl.when(has_high)(down.wait_recv)
        pl.when(has_low)(up.wait_recv)

    def wait_send(self, flows):
        for copy, has in flows:
            pl.when(has)(copy.wait_send)

    def zero_edges(self, name, halos):
        for side, at in ((0, 0), (1, self.sizes[name] - 1)):
            @pl.when(self.pos[name] == at)
            def _():
                for slot in range(2):
                    halos[slot, side] = jnp.zeros(halos.shape[2:], halos.dtype)

    def x_edge(self, src, xh, sems, slot, lanes):
        send, recv = sems
        me = self.pos['gx']
        first = pl.multiple_of((1 - me) * (lanes - TILE), TILE)
        return pltpu.make_async_remote_copy(src.at[:, :, pl.ds(first, TILE)], xh.at[slot], send, recv.at[slot], device_id={'gx': 1 - me}, device_id_type=MESH)


def y_flows(links, buf, halos, sems, slot, tile):
    cols = lane_ds(tile)
    ny, half = buf.shape[0], halos.shape[2]
    dst = [halos.at[slot, side, :, :, cols] for side in range(2)]
    return links.pair('gy', buf.at[pl.ds(0, half), :, cols], buf.at[pl.ds(ny - half, half), :, cols], dst, sems, slot, tile)


def z_flows(links, zs, zr, sems, slot, tile):
    cols = lane_ds(tile)
    dst = [zr.at[slot, side, :, :, cols] for side in range(2)]
    return links.pair('gz', zs.at[0, :, :, cols], zs.at[1, :, :, cols], dst, sems, slot, tile)


def dot(a, b):
    return jnp.dot(a, b, preferred_element_type=F32)


def x_stage(src, xh, wx, me, layer, slot, tile, outer, edge, before_edge, emit):
    ny, nz, lanes = src.shape
    count = 8
    far, near = lanes - 2 * TILE, 0

    def rows(y, lane, width, weight):
        block = src[pl.ds(y, count), :, pl.ds(pl.multiple_of(lane, TILE), width)]
        return dot(block.reshape(count * nz, width), weight)

    @pl.when(outer)
    def _():
        weight = wx[layer, pl.ds(pl.multiple_of((1 - me) * TILE, TILE), 2 * TILE), :]
        for y in range(0, ny, count):
            emit(y, count, rows(y, me * far, 2 * TILE, weight))

    @pl.when(jnp.logical_not(outer | edge))
    def _():
        weight = wx[layer]
        for y in range(0, ny, count):
            emit(y, count, rows(y, (tile - 1) * TILE, 3 * TILE, weight))

    @pl.when(edge)
    def _():
        before_edge()
        weight = wx[layer, pl.ds(pl.multiple_of(me * TILE, TILE), 2 * TILE), :]
        other = wx[layer, pl.ds(pl.multiple_of((1 - me) * 2 * TILE, TILE), TILE), :]
        for y in range(0, ny, count):
            outside = dot(xh[slot, pl.ds(y, count)].reshape(count * nz, TILE), other)
            emit(y, count, rows(y, (1 - me) * far, 2 * TILE, weight) + outside)


def y_stage(src, halos, ly, layer, slot, tile, picks, emit):
    ny, nz, lanes, tiles, group, ysub = dims(src.shape, halos.shape[2])
    half = halos.shape[2]
    cols = lane_ds(tile)
    main = group * ROWS
    base = ly[layer, pl.ds(0, main), :]
    low = ly[layer, pl.ds(0, main + 2 * ROWS), :]
    high = jnp.concatenate([base, ly[layer, pl.ds(main + 2 * ROWS, 2 * ROWS), :]], axis=0)
    for g in range(ny // group):
        for zb in range(nz // ROWS):
            zrows = pl.ds(zb * ROWS, ROWS)
            first, last = g * group - half, g * group - half + ROWS
            parts = []
            if first < 0:
                parts.append(halos[slot, 0, :, zrows, cols])
            parts.append(src[pl.ds(max(first, 0), min(last, ny) - max(first, 0)), zrows, cols])
            if last > ny:
                parts.append(halos[slot, 1, :, zrows, cols])
            rhs = jnp.concatenate(parts, axis=0) if len(parts) > 1 else parts[0]
            side = {0: 0, nz // ROWS - 1: 1}.get(zb) if picks else None
            lhs = {None: base, 0: low, 1: high}[side]
            emit(g, zb, side, dot(lhs, rhs.reshape(ROWS * ROWS, TILE)).astype(BF16))


def z_stage(src, zr, lz, layer, slot, tile, ysub, emit):
    ny, nz, lanes = src.shape
    cols = lane_ds(tile)
    lhs = lz[layer]
    for g in range(ny // ysub):
        main = src[pl.ds(g * ysub, ysub), :, cols].reshape(ysub * nz, TILE)
        rhs = jnp.concatenate([main, zr[slot, 0, g, :, cols], zr[slot, 1, g, :, cols]], axis=0)
        emit(g, dot(lhs, rhs).astype(BF16).reshape(ysub, nz, TILE))


def fwd_kernel(half, sizes, v_hbm, wx, ly, lz, wd, bias, a3_hbm, vol, xh, a1, yr, a2, zs, zr, a3, in_sem, out_sem, xsend, xrecv, ysend, yrecv, zsend, zrecv):
    ny, nz, lanes, tiles, group, ysub = dims(v_hbm.shape, half)
    layers = wx.shape[0]
    links = Links(sizes)
    me = links.pos['gx']
    ysems, zsems, xsems = (ysend, yrecv), (zsend, zrecv), (xsend, xrecv)
    total = layers * tiles
    lag_y, lag_z = 2, 4
    assert lag_z <= tiles - 2

    def place(item):
        layer, p = item // tiles, lax.rem(item, tiles)
        return layer, p, p + me * (tiles - 1 - 2 * p), lax.rem(layer, 2)

    def fetch(tile):
        return pltpu.make_async_copy(v_hbm.at[:, :, lane_ds(tile)], vol.at[:, :, lane_ds(tile)], in_sem.at[tile])

    def put(layer, tile):
        return pltpu.make_async_copy(a3.at[:, :, lane_ds(tile)], a3_hbm.at[layer, :, :, lane_ds(tile)], out_sem.at[tile])

    def y_at(slot, tile):
        return y_flows(links, a1, yr, ysems, slot, tile)

    def z_at(slot, tile):
        return z_flows(links, zs, zr, zsems, slot, tile)

    def x_at(slot):
        return links.x_edge(vol, xh, xsems, slot, lanes)

    edge_tile = place(tiles - 1)[2]
    fetch(edge_tile).start()
    for p in range(tiles - 1):
        fetch(place(p)[2]).start()
    links.zero_edges('gy', yr)
    links.zero_edges('gz', zr)
    links.barrier()
    fetch(edge_tile).wait()
    x_at(0).start()

    @pl.loop(0, total + lag_z)
    def _(step):
        @pl.when(step < total)
        def _():
            layer, p, tile, slot = place(step)

            @pl.when(layer == 0)
            def _():
                pl.when(p == 0)(fetch(tile).wait)
                pl.when(p < tiles - 2)(fetch(place(p + 1)[2]).wait)

            @pl.when(layer > 0)
            def _():
                links.wait_send(y_at(1 - slot, tile))

            def before_edge():
                x_at(slot).wait_recv()
                x_at(slot).wait_send()

            def emit(y, count, out):
                a1[pl.ds(y, count), :, lane_ds(tile)] = out.astype(BF16).reshape(count, nz, TILE)

            x_stage(vol, xh, wx, me, layer, slot, tile, p == 0, p == tiles - 1, before_edge, emit)
            links.start(y_at(slot, tile))

        @pl.when((step >= lag_y) & (step < total + lag_y))
        def _():
            layer, p, tile, slot = place(step - lag_y)
            cols = lane_ds(tile)

            @pl.when(layer > 0)
            def _():
                links.wait_send(z_at(1 - slot, tile))

            links.wait_recv(y_at(slot, tile))

            def emit(g, zb, side, out):
                a2[pl.ds(g * group, group), pl.ds(zb * ROWS, ROWS), cols] = out[: group * ROWS].reshape(group, ROWS, TILE)
                if side is not None:
                    zs[side, pl.ds(2 * g, 2), :, cols] = out[group * ROWS :].reshape(2, ROWS, TILE)

            y_stage(a1, yr, ly, layer, slot, tile, True, emit)
            links.start(z_at(slot, tile))

        @pl.when(step >= lag_z)
        def _():
            layer, p, tile, slot = place(step - lag_z)
            cols = lane_ds(tile)

            @pl.when(layer > 0)
            def _():
                put(layer - 1, tile).wait()

            links.wait_recv(z_at(slot, tile))

            def emit(g, out):
                a3[pl.ds(g * ysub, ysub), :, cols] = out

            z_stage(a2, zr, lz, layer, slot, tile, ysub, emit)
            put(layer, tile).start()

            @pl.when(layer < layers - 1)
            def _():
                for g in range(ny // group):
                    rows = pl.ds(g * group, group)
                    pre = dot(a3[rows, :, cols].reshape(group * nz, TILE), wd[layer]) + bias[layer]
                    old = vol[rows, :, cols].astype(F32).reshape(group * nz, TILE)
                    new = old + (0.5 * pre) * (1.0 + lax.erf(pre * INV_SQRT2))
                    vol[rows, :, cols] = new.astype(BF16).reshape(group, nz, TILE)
                pl.when(p == tiles - 1)(x_at(1 - slot).start)

    @pl.loop(0, tiles)
    def _(tile):
        slot = (layers - 1) % 2
        links.wait_send(y_at(slot, tile))
        links.wait_send(z_at(slot, tile))
        put(layers - 1, tile).wait()


def bwd_kernel(half, sizes, chans, a3_hbm, g_hbm, wx, ly, lz, pick, wd, wt, bias, go_hbm, sums, acts, grad, sb, d3, zs, zr, d2, yr, d1, xh, dw, db, gathered, act_sem, in_sem, out_sem, gsend, grecv, xsend, xrecv, ysend, yrecv, zsend, zrecv):
    ny, nz, lanes, tiles, group, ysub = dims(g_hbm.shape, half)
    layers = wx.shape[0]
    links = Links(sizes)
    me = links.pos['gx']
    ysems, zsems, xsems = (ysend, yrecv), (zsend, zrecv), (xsend, xrecv)
    total = layers * tiles
    lag_z, lag_y, lag_x = 2, 4, 5
    ahead = acts.shape[0] - 1
    assert lag_x <= tiles - 1

    def place(item):
        turn, p = item // tiles, lax.rem(item, tiles)
        tile = (tiles - 1 - p) + me * (2 * p - tiles + 1)
        return layers - 1 - turn, turn, p, tile, lax.rem(turn, 2)

    def fetch(item):
        layer, turn, p, tile, slot = place(item)
        ring = lax.rem(item, ahead + 1)
        return pltpu.make_async_copy(a3_hbm.at[layer, :, :, lane_ds(tile)], acts.at[ring], act_sem.at[ring])

    def load(tile):
        return pltpu.make_async_copy(g_hbm.at[:, :, lane_ds(tile)], grad.at[:, :, lane_ds(tile)], in_sem.at[tile])

    def put(tile):
        return pltpu.make_async_copy(grad.at[:, :, lane_ds(tile)], go_hbm.at[:, :, lane_ds(tile)], out_sem.at[tile])

    def y_at(slot, tile):
        return y_flows(links, d2, yr, ysems, slot, tile)

    def z_at(slot, tile):
        return z_flows(links, zs, zr, zsems, slot, tile)

    def x_at(slot):
        return links.x_edge(d1, xh, xsems, slot, lanes)

    rounds = []
    for name, size in sizes.items():
        bit = 1
        while bit < size:
            rounds.append((name, bit))
            bit *= 2
    assert len(rounds) <= lag_x

    def share(index):
        name, bit = rounds[index]
        pos = links.pos[name]
        other = pos + bit - 2 * bit * lax.rem(pos // bit, 2)
        return pltpu.make_async_remote_copy(sums, gathered.at[index], gsend.at[index], grecv.at[index], device_id={name: other}, device_id_type=MESH)

    def finish(index):
        share(index).wait_send()
        share(index).wait_recv()
        sums[...] = sums[...] + gathered[index]

    for item in range(ahead):
        fetch(item).start()
        load(place(item)[3]).start()
    for item in range(ahead, tiles):
        load(place(item)[3]).start()
    links.zero_edges('gy', yr)
    links.zero_edges('gz', zr)
    links.barrier()

    @pl.loop(0, total + lag_x)
    def _(step):
        @pl.when((step >= lag_z) & (step < total + lag_z))
        def _():
            layer, turn, p, tile, slot = place(step - lag_z)
            cols = lane_ds(tile)

            @pl.when(turn > 0)
            def _():
                links.wait_send(y_at(1 - slot, tile))

            links.wait_recv(z_at(slot, tile))

            def emit(g, out):
                d2[pl.ds(g * ysub, ysub), :, cols] = out

            z_stage(d3, zr, lz, layer, slot, tile, ysub, emit)
            links.start(y_at(slot, tile))

        @pl.when((step >= lag_y) & (step < total + lag_y))
        def _():
            layer, turn, p, tile, slot = place(step - lag_y)
            cols = lane_ds(tile)
            links.wait_recv(y_at(slot, tile))

            def emit(g, zb, side, out):
                d1[pl.ds(g * group, group), pl.ds(zb * ROWS, ROWS), cols] = out.reshape(group, ROWS, TILE)

            y_stage(d2, yr, ly, layer, slot, tile, False, emit)
            pl.when(p == 0)(x_at(slot).start)

        @pl.when(step >= lag_x)
        def _():
            layer, turn, p, tile, slot = place(step - lag_x)
            cols = lane_ds(tile)

            def before_edge():
                x_at(slot).wait_recv()
                x_at(slot).wait_send()

            def emit(y, count, out):
                rows = pl.ds(y, count)
                old = grad[rows, :, cols].astype(F32).reshape(count * nz, TILE)
                grad[rows, :, cols] = (old + out).astype(BF16).reshape(count, nz, TILE)

            x_stage(d1, xh, wx, me, layer, slot, tile, p == tiles - 1, p == 0, before_edge, emit)
            pl.when(layer == 0)(put(tile).start)

        @pl.when(step < total)
        def _():
            layer, turn, p, tile, slot = place(step)
            cols = lane_ds(tile)
            ring = lax.rem(step, ahead + 1)
            fetch(step).wait()

            @pl.when(step + ahead < total)
            def _():
                fetch(step + ahead).start()

            @pl.when(turn == 0)
            def _():
                load(tile).wait()

            @pl.when(turn > 0)
            def _():
                links.wait_send(z_at(1 - slot, tile))

            @pl.when(p == 0)
            def _():
                dw[...] = jnp.zeros_like(dw)
                db[...] = jnp.zeros_like(db)

            span = ysub * nz
            totals = jnp.zeros((8, TILE), F32)
            for g in range(ny // ysub):
                rows = pl.ds(g * ysub, ysub)
                pre = dot(acts[ring, rows].reshape(span, TILE), wd[layer]) + bias[layer]
                cot = grad[rows, :, cols].astype(F32).reshape(span, TILE)
                root = pre * INV_SQRT2
                bell = jnp.exp(-(root * root))
                scaled = (0.5 * cot) * ((1.0 + lax.erf(root)) + (root * TWO_INV_SQRT_PI) * bell)
                totals = totals + jnp.sum(scaled.reshape(span // 8, 8, TILE), axis=0)
                sb[pl.ds(g * span, span), :] = scaled.astype(BF16)
            db[...] += totals
            for g in range(ny // ysub):
                mixed = dot(sb[pl.ds(g * span, span), :], wt[layer]).astype(BF16)
                d3[pl.ds(g * ysub, ysub), :, cols] = mixed.reshape(ysub, nz, TILE)
                planes = dot(pick[...], mixed).astype(BF16)
                zs[0, g, :, cols] = planes[:ROWS]
                zs[1, g, :, cols] = planes[ROWS:]
            links.start(z_at(slot, tile))
            dw[...] += lax.dot_general(acts[ring].reshape(ny * nz, TILE), sb[...], (((0,), (0,)), ((), ())), preferred_element_type=F32)

            @pl.when(p == tiles - 1)
            def _():
                lane = lax.broadcasted_iota(jnp.int32, (chans, TILE), 1) // chans
                diag = jnp.zeros((chans, TILE), F32)
                for i in range(TILE // chans):
                    diag = diag + jnp.where(lane == i, dw[pl.ds(i * chans, chans), :], 0.0)
                sums[layer, pl.ds(0, chans), :] = diag
                sums[layer, pl.ds(chans, 8), :] = db[...]

        for index in range(len(rounds)):
            @pl.when(step == total + index)
            def _():
                if index > 0:
                    finish(index - 1)
                share(index).start()

    finish(len(rounds) - 1)

    @pl.loop(0, tiles)
    def _(tile):
        slot = (layers - 1) % 2
        links.wait_send(y_at(slot, tile))
        links.wait_send(z_at(slot, tile))
        put(tile).wait()


def link_sems(tiles):
    dma = pltpu.SemaphoreType.DMA
    return [dma, dma((2,)), dma((2, tiles)), dma((2, 2, tiles)), dma((2, tiles)), dma((2, 2, tiles))]


def solution(mesh):
    names = ('gx', 'gy', 'gz')
    sizes = {name: mesh.shape[name] for name in names}
    vol_spec = P('dp', 'gx', 'gy', 'gz')
    any_spec = pl.BlockSpec(memory_space=pl.ANY)
    vmem_spec = pl.BlockSpec(memory_space=pltpu.VMEM)
    dma = pltpu.SemaphoreType.DMA

    def local_step(volume, cot_out, filter_taps, w_mix, b_mix):
        chans, nx, ny, nz = volume.shape
        layers, _, num_taps = filter_taps.shape
        half = (num_taps - 1) // 2
        lanes = nx * chans
        tiles = lanes // TILE
        reps = TILE // chans
        ysub = (ROWS - 2 * half) // 2
        params = functools.partial(pltpu.CompilerParams, has_side_effects=True, vmem_limit_bytes=VMEM_BYTES)
        wx_f, wx_b, ly_f, ly_b, lz_f, lz_b, wd, wt = band_weights(filter_taps, w_mix, ysub, nz)
        pick = pick_matrix(half, ysub, nz)
        bias = jnp.tile(b_mix, (1, reps))[:, None, :]

        full = pltpu.VMEM((ny, nz, lanes), BF16)
        one = (ny, nz, TILE)
        two = pltpu.VMEM((2,) + one, BF16)
        y_halo = pltpu.VMEM((2, 2, half, nz, lanes), BF16)
        z_send = pltpu.VMEM((2, ny // ysub, ROWS, lanes), BF16)
        z_halo = pltpu.VMEM((2, 2, ny // ysub, ROWS, lanes), BF16)

        acts = pl.pallas_call(
            functools.partial(fwd_kernel, half, sizes),
            out_shape=jax.ShapeDtypeStruct((layers, ny, nz, lanes), BF16),
            in_specs=[any_spec] + [vmem_spec] * 5,
            out_specs=any_spec,
            scratch_shapes=[full, two, full, y_halo, full, z_send, z_halo, full, dma((tiles,)), dma((tiles,))] + link_sems(tiles),
            compiler_params=params(collective_id=0),
            name='fwd_layers',
        )(to_dense(volume), wx_f, ly_f, lz_f, wd, bias)
        rounds = sum((size - 1).bit_length() for size in sizes.values())
        sum_shape = (layers, chans + 8, TILE)
        grad, sums = pl.pallas_call(
            functools.partial(bwd_kernel, half, sizes, chans),
            out_shape=[jax.ShapeDtypeStruct((ny, nz, lanes), BF16), jax.ShapeDtypeStruct(sum_shape, F32)],
            in_specs=[any_spec] * 2 + [vmem_spec] * 7,
            out_specs=[any_spec, vmem_spec],
            scratch_shapes=[pltpu.VMEM((3,) + one, BF16), full, pltpu.VMEM((ny * nz, TILE), BF16), full, z_send, z_halo, full, y_halo, full, two]
            + [pltpu.VMEM((TILE, TILE), F32), pltpu.VMEM((8, TILE), F32), pltpu.VMEM((rounds,) + sum_shape, F32)]
            + [dma((3,)), dma((tiles,)), dma((tiles,)), dma((rounds,)), dma((rounds,))]
            + link_sems(tiles),
            compiler_params=params(collective_id=1),
            name='bwd_layers',
        )(acts, to_dense(cot_out), wx_b, ly_b, lz_b, pick, wd, wt, bias)
        blocks = sums.reshape(layers, chans + 8, reps, chans).sum(axis=2)
        return from_dense(grad, chans), blocks[:, :chans], blocks[:, chans:].sum(axis=1)

    return jax.shard_map(local_step, mesh=mesh, in_specs=(vol_spec, vol_spec, P(), P(), P()), out_specs=(vol_spec, P('dp'), P('dp')), check_vma=False)
```

time: 392 us -> 294 us (0.75)
  blocking collectives: 45.1 us -> 0 us
  Pallas kernels: 333 us -> 288 us
  local copies, waits for them, and re-layouts: 12.3 us -> 2.13 us
    pallas_call x6 -> x2, Pallas kernels: 264 us -> 218 us  [the longest x1 146 us: local_step(): pl.pallas_call(functools.partial(bwd_kernel, half, sizes, chans), out_sha...]
    psum x1 -> x0, blocking collectives: 45.1 us -> none  [local_step(): grad_w_sum = lax.psum(jnp.stack(grad_w), names)]
    squeeze x4 -> x0, local copies, waits for them, and re-layouts: 8.99 us -> none  [the longest x1 3.15 us: local_step(): wx_b[layer]]
where the time goes in v3:
time: 294 us; the launch traced here: 291 us
  Pallas kernels  288 us (98%)
    pallas_call x1, Pallas kernels, local_step(): pl.pallas_call(functools.partial(bwd_kernel, half, sizes, chans), out_sha...  146 us
    pallas_call x1, Pallas kernels, local_step(): pl.pallas_call(functools.partial(fwd_kernel, half, sizes), out_shape=jax....  71.9 us
    pallas_call x2, Pallas kernels, to_dense(): pl.pallas_call(entry_kernel, grid=(ny // SUB,), in_specs=[pl.BlockSpec((c...  40.5 us
    pallas_call x1, Pallas kernels, from_dense(): pl.pallas_call(leave_kernel, grid=(ny // SUB,), in_specs=[pl.BlockSpec((S...  20.7 us
    pallas_call x1, Pallas kernels, band_weights(): pl.pallas_call(band_kernel, out_shape=[jax.ShapeDtypeStruct((layers,) + s...  8.24 us

profile of v3, /device:TPU:97, one launch (start us, length us, event | category | flops | bytes accessed | tf_op | source)
XLA Modules:
  0.0 291.3 jit_solution(8979180292215844629)
XLA Ops:
  0.6 8.2 %band_weights.1 = (bf16[3,768,256]{2,1,0:T(8,128)(2,1)}, bf16[3,768,256]{2,1,0:T(8,128)(2,1)}, bf16[3,160,256]{2,1,0:T(8,128)(2,1)}, bf16[3,160,256]{2,1,0:T(8,1...) custom-call(f32[3,3,11]{2,1,0:T(4,128)} %taps.1, ...), custom_call_target="tpu_custom_call" | custom-call | tf_op jit(solution)/shard_map/band_weights/pallas_call | solution.py:107
  8.9 0.7 tile.8
  9.6 0.7 tile.9.bias
  10.2 20.2 %to_dense.2.v_hbm = bf16[48,48,1536]{2,1,0:T(8,128)(2,1)} custom-call(bf16[32,48,48,48]{3,2,1,0:T(8,128)(2,1)} %src.2), custom_call_target="tpu_custom_call" | custom-call | tf_op jit(solution)/shard_map/to_dense/pallas_call | solution.py:137
  30.4 71.9 %fwd_layers.1.a3_hbm = bf16[3,48,48,1536]{3,2,1,0:T(8,128)(2,1)} custom-call(bf16[48,48,1536]{2,1,0:T(8,128)(2,1)} %to_dense.2.v_hbm, bf16[3,768,256]{2,1,0:T(8,128)(2,1)} %get-tuple-element.13.wx, bf16[3,160,256]{2,1,0:T(8,128)(2,1)} %get-tuple-element.14.ly, bf16[3,144,176]{2,1,0:T(8,128)(2,1)} %get-tuple-element.15.lz, ...), custom_call_target="tpu_custom_call" | custom-call | tf_op jit(solution)/shard_map/fwd_layers/pallas_call | solution.py:658
  102.4 20.2 %to_dense.3.g_hbm = bf16[48,48,1536]{2,1,0:T(8,128)(2,1)} custom-call(bf16[32,48,48,48]{3,2,1,0:T(8,128)(2,1)} %src.3), custom_call_target="tpu_custom_call" | custom-call | tf_op jit(solution)/shard_map/to_dense/pallas_call | solution.py:137
  122.6 146.4 %bwd_layers.1 = (bf16[48,48,1536]{2,1,0:T(8,128)(2,1)}, f32[3,40,256]{2,1,0:T(8,128)}) custom-call(bf16[3,48,48,1536]{3,2,1,0:T(8,128)(2,1)} %fwd_layers.1.a3_hbm, bf16[48,48,1536]{2,1,0:T(8,128)(2,1)} %to_dense.3.g_hbm, bf16[3,768,256]{2,1,0:T(8,128)(2,1)} %get-tuple-element.17.wx, bf16[3,160,256]{2,1,0:T(8,128)(2,1)} %get-tuple-element.18.ly, ...), custom_call_target="tpu_custom_call" | custom-call | tf_op jit(solution)/shard_map/bwd_layers/pallas_call | solution.py:669
  269.0 0.0 copy-start
  269.0 20.7 %from_dense.1 = bf16[32,48,48,48]{3,2,1,0:T(8,128)(2,1)} custom-call(bf16[48,48,1536]{2,1,0:T(8,128)(2,1)} %get-tuple-element.21.src), custom_call_target="tpu_custom_call" | custom-call | tf_op jit(solution)/shard_map/from_dense/pallas_call | solution.py:172
  289.7 0.0 copy-done
  289.7 0.2 reshape.15
  289.9 0.1 reduce_sum.18
  290.0 0.6 slice.8
  290.7 0.6 slice_reduce_fusion
Async XLA Ops:
  269.0 20.7 %copy-start = (f32[3,40,256]{2,1,0:T(8,128)S(1)}, f32[3,40,256]{2,1,0:T(8,128)}, u32[]{:S(2)}) copy-start(f32[3,40,256]{2,1,0:T(8,128)} %get-tuple-element.22) | copy-start | bytes 368644

commit v4 on v3

--- a/solution.py
+++ b/solution.py
@@ -15,6 +15,7 @@
 SUB = 8
 VMEM_BYTES = 60 * 1024 * 1024
 INV_SQRT2 = 0.7071067811865476
+NEG_LOG2E = -1.4426950408889634
 TWO_INV_SQRT_PI = 1.1283791670955126
 F32 = jnp.float32
 BF16 = jnp.bfloat16
@@ -415,21 +416,36 @@
 
             links.wait_recv(z_at(slot, tile))
 
+            groups = ny // ysub
+
             def emit(g, out):
                 a3[pl.ds(g * ysub, ysub), :, cols] = out
 
-            z_stage(a2, zr, lz, layer, slot, tile, ysub, emit)
+            @pl.when(layer == layers - 1)
+            def _():
+                z_stage(a2, zr, lz, layer, slot, tile, ysub, emit)
+
+            @pl.when(layer < layers - 1)
+            def _():
+                held = {}
+
+                def mix_and_update(g, out):
+                    if out is not None:
+                        emit(g, out)
+                        held[g] = dot(out.reshape(ysub * nz, TILE), wd[layer])
+                    if g >= 1:
+                        mix = held.pop(g - 1)
+                        for i in range(ysub):
+                            y = (g - 1) * ysub + i
+                            pre = mix[i * nz : (i + 1) * nz] + bias[layer]
+                            new = vol[y, :, cols].astype(F32) + (0.5 * pre) * (1.0 + lax.erf(pre * INV_SQRT2))
+                            vol[y, :, cols] = new.astype(BF16)
+
+                z_stage(a2, zr, lz, layer, slot, tile, ysub, mix_and_update)
+                mix_and_update(groups, None)
+                pl.when(p == tiles - 1)(x_at(1 - slot).start)
+
             put(layer, tile).start()
-
-            @pl.when(layer < layers - 1)
-            def _():
-                for g in range(ny // group):
-                    rows = pl.ds(g * group, group)
-                    pre = dot(a3[rows, :, cols].reshape(group * nz, TILE), wd[layer]) + bias[layer]
-                    old = vol[rows, :, cols].astype(F32).reshape(group * nz, TILE)
-                    new = old + (0.5 * pre) * (1.0 + lax.erf(pre * INV_SQRT2))
-                    vol[rows, :, cols] = new.astype(BF16).reshape(group, nz, TILE)
-                pl.when(p == tiles - 1)(x_at(1 - slot).start)
 
     @pl.loop(0, tiles)
     def _(tile):
@@ -446,9 +462,9 @@
     me = links.pos['gx']
     ysems, zsems, xsems = (ysend, yrecv), (zsend, zrecv), (xsend, xrecv)
     total = layers * tiles
-    lag_z, lag_y, lag_x = 2, 4, 5
+    lag_z, lag_y, lag_x = 2, 5, 6
     ahead = acts.shape[0] - 1
-    assert lag_x <= tiles - 1
+    assert lag_x <= tiles
 
     def place(item):
         turn, p = item // tiles, lax.rem(item, tiles)
@@ -505,23 +521,6 @@
 
     @pl.loop(0, total + lag_x)
     def _(step):
-        @pl.when((step >= lag_z) & (step < total + lag_z))
-        def _():
-            layer, turn, p, tile, slot = place(step - lag_z)
-            cols = lane_ds(tile)
-
-            @pl.when(turn > 0)
-            def _():
-                links.wait_send(y_at(1 - slot, tile))
-
-            links.wait_recv(z_at(slot, tile))
-
-            def emit(g, out):
-                d2[pl.ds(g * ysub, ysub), :, cols] = out
-
-            z_stage(d3, zr, lz, layer, slot, tile, ysub, emit)
-            links.start(y_at(slot, tile))
-
         @pl.when((step >= lag_y) & (step < total + lag_y))
         def _():
             layer, turn, p, tile, slot = place(step - lag_y)
@@ -576,23 +575,34 @@
                 db[...] = jnp.zeros_like(db)
 
             span = ysub * nz
+            groups = ny // ysub
+
+            def mix_of(g):
+                return dot(acts[ring, pl.ds(g * ysub, ysub)].reshape(span, TILE), wd[layer])
+
             totals = jnp.zeros((8, TILE), F32)
-            for g in range(ny // ysub):
-                rows = pl.ds(g * ysub, ysub)
-                pre = dot(acts[ring, rows].reshape(span, TILE), wd[layer]) + bias[layer]
-                cot = grad[rows, :, cols].astype(F32).reshape(span, TILE)
-                root = pre * INV_SQRT2
-                bell = jnp.exp(-(root * root))
-                scaled = (0.5 * cot) * ((1.0 + lax.erf(root)) + (root * TWO_INV_SQRT_PI) * bell)
-                totals = totals + jnp.sum(scaled.reshape(span // 8, 8, TILE), axis=0)
-                sb[pl.ds(g * span, span), :] = scaled.astype(BF16)
+            mix, mixed = mix_of(0), {}
+            for g in range(groups + 2):
+                following = mix_of(g + 1) if g + 1 < groups else None
+                if 1 <= g <= groups:
+                    mixed[g - 1] = dot(sb[pl.ds((g - 1) * span, span), :], wt[layer]).astype(BF16)
+                    d3[pl.ds((g - 1) * ysub, ysub), :, cols] = mixed[g - 1].reshape(ysub, nz, TILE)
+                if g >= 2:
+                    planes = dot(pick[...], mixed.pop(g - 2)).astype(BF16)
+                    zs[0, g - 2, :, cols] = planes[:ROWS]
+                    zs[1, g - 2, :, cols] = planes[ROWS:]
+                if g < groups:
+                    for i in range(ysub):
+                        y = g * ysub + i
+                        pre = mix[i * nz : (i + 1) * nz] + bias[layer]
+                        cot = grad[y, :, cols].astype(F32)
+                        root = pre * INV_SQRT2
+                        bell = jnp.exp2((root * root) * NEG_LOG2E)
+                        scaled = (0.5 * cot) * ((1.0 + lax.erf(root)) + (root * TWO_INV_SQRT_PI) * bell)
+                        totals = totals + jnp.sum(scaled.reshape(nz // 8, 8, TILE), axis=0)
+                        sb[pl.ds(y * nz, nz), :] = scaled.astype(BF16)
+                mix = following
             db[...] += totals
-            for g in range(ny // ysub):
-                mixed = dot(sb[pl.ds(g * span, span), :], wt[layer]).astype(BF16)
-                d3[pl.ds(g * ysub, ysub), :, cols] = mixed.reshape(ysub, nz, TILE)
-                planes = dot(pick[...], mixed).astype(BF16)
-                zs[0, g, :, cols] = planes[:ROWS]
-                zs[1, g, :, cols] = planes[ROWS:]
             links.start(z_at(slot, tile))
             dw[...] += lax.dot_general(acts[ring].reshape(ny * nz, TILE), sb[...], (((0,), (0,)), ((), ())), preferred_element_type=F32)
 
@@ -604,6 +614,23 @@
                     diag = diag + jnp.where(lane == i, dw[pl.ds(i * chans, chans), :], 0.0)
                 sums[layer, pl.ds(0, chans), :] = diag
                 sums[layer, pl.ds(chans, 8), :] = db[...]
+
+        @pl.when((step >= lag_z) & (step < total + lag_z))
+        def _():
+            layer, turn, p, tile, slot = place(step - lag_z)
+            cols = lane_ds(tile)
+
+            @pl.when(turn > 0)
+            def _():
+                links.wait_send(y_at(1 - slot, tile))
+
+            links.wait_recv(z_at(slot, tile))
+
+            def emit(g, out):
+                d2[pl.ds(g * ysub, ysub), :, cols] = out
+
+            z_stage(d3, zr, lz, layer, slot, tile, ysub, emit)
+            links.start(y_at(slot, tile))
 
         for index in range(len(rounds)):
             @pl.when(step == total + index)

time: 294 us -> 251 us (0.85)
  Pallas kernels: 288 us -> 246 us
    pallas_call x1, Pallas kernels: 146 us -> 107 us  [local_step(): pl.pallas_call(functools.partial(bwd_kernel, half, sizes, chans), out_sha...]
where the time goes in v4:
time: 251 us; the launch traced here: 249 us
  Pallas kernels  246 us (98%)
    pallas_call x1, Pallas kernels, local_step(): pl.pallas_call(functools.partial(bwd_kernel, half, sizes, chans), out_sha...  107 us
    pallas_call x1, Pallas kernels, local_step(): pl.pallas_call(functools.partial(fwd_kernel, half, sizes), out_shape=jax....  69.3 us
    pallas_call x2, Pallas kernels, to_dense(): pl.pallas_call(entry_kernel, grid=(ny // SUB,), in_specs=[pl.BlockSpec((c...  40.5 us
    pallas_call x1, Pallas kernels, from_dense(): pl.pallas_call(leave_kernel, grid=(ny // SUB,), in_specs=[pl.BlockSpec((S...  20.7 us
    pallas_call x1, Pallas kernels, band_weights(): pl.pallas_call(band_kernel, out_shape=[jax.ShapeDtypeStruct((layers,) + s...  8.24 us

profile of v4, /device:TPU:97, one launch (start us, length us, event | category | flops | bytes accessed | tf_op | source)
XLA Modules:
  0.0 249.1 jit_solution(17441708774615847288)
XLA Ops:
  0.6 8.2 %band_weights.1 = (bf16[3,768,256]{2,1,0:T(8,128)(2,1)}, bf16[3,768,256]{2,1,0:T(8,128)(2,1)}, bf16[3,160,256]{2,1,0:T(8,128)(2,1)}, bf16[3,160,256]{2,1,0:T(8,1...) custom-call(f32[3,3,11]{2,1,0:T(4,128)} %taps.1, ...), custom_call_target="tpu_custom_call" | custom-call | tf_op jit(solution)/shard_map/band_weights/pallas_call | solution.py:108
  8.9 0.7 tile.8
  9.6 0.7 tile.9.bias
  10.2 20.2 %to_dense.2.v_hbm = bf16[48,48,1536]{2,1,0:T(8,128)(2,1)} custom-call(bf16[32,48,48,48]{3,2,1,0:T(8,128)(2,1)} %src.2), custom_call_target="tpu_custom_call" | custom-call | tf_op jit(solution)/shard_map/to_dense/pallas_call | solution.py:138
  30.4 69.3 %fwd_layers.1.a3_hbm = bf16[3,48,48,1536]{3,2,1,0:T(8,128)(2,1)} custom-call(bf16[48,48,1536]{2,1,0:T(8,128)(2,1)} %to_dense.2.v_hbm, bf16[3,768,256]{2,1,0:T(8,128)(2,1)} %get-tuple-element.13.wx, bf16[3,160,256]{2,1,0:T(8,128)(2,1)} %get-tuple-element.14.ly, bf16[3,144,176]{2,1,0:T(8,128)(2,1)} %get-tuple-element.15.lz, ...), custom_call_target="tpu_custom_call" | custom-call | tf_op jit(solution)/shard_map/fwd_layers/pallas_call | solution.py:685
  99.8 20.2 %to_dense.3.g_hbm = bf16[48,48,1536]{2,1,0:T(8,128)(2,1)} custom-call(bf16[32,48,48,48]{3,2,1,0:T(8,128)(2,1)} %src.3), custom_call_target="tpu_custom_call" | custom-call | tf_op jit(solution)/shard_map/to_dense/pallas_call | solution.py:138
  120.0 106.9 %bwd_layers.1 = (bf16[48,48,1536]{2,1,0:T(8,128)(2,1)}, f32[3,40,256]{2,1,0:T(8,128)}) custom-call(bf16[3,48,48,1536]{3,2,1,0:T(8,128)(2,1)} %fwd_layers.1.a3_hbm, bf16[48,48,1536]{2,1,0:T(8,128)(2,1)} %to_dense.3.g_hbm, bf16[3,768,256]{2,1,0:T(8,128)(2,1)} %get-tuple-element.17.wx, bf16[3,160,256]{2,1,0:T(8,128)(2,1)} %get-tuple-element.18.ly, ...), custom_call_target="tpu_custom_call" | custom-call | tf_op jit(solution)/shard_map/bwd_layers/pallas_call | solution.py:696
  226.9 0.0 copy-start
  226.9 20.7 %from_dense.1 = bf16[32,48,48,48]{3,2,1,0:T(8,128)(2,1)} custom-call(bf16[48,48,1536]{2,1,0:T(8,128)(2,1)} %get-tuple-element.21.src), custom_call_target="tpu_custom_call" | custom-call | tf_op jit(solution)/shard_map/from_dense/pallas_call | solution.py:173
  247.6 0.0 copy-done
  247.6 0.2 reshape.15
  247.8 0.1 reduce_sum.18
  247.9 0.6 slice.8
  248.6 0.6 slice_reduce_fusion
Async XLA Ops:
  226.9 20.7 %copy-start = (f32[3,40,256]{2,1,0:T(8,128)S(1)}, f32[3,40,256]{2,1,0:T(8,128)}, u32[]{:S(2)}) copy-start(f32[3,40,256]{2,1,0:T(8,128)} %get-tuple-element.22) | copy-start | bytes 368644

commit v5 on v4

--- a/solution.py
+++ b/solution.py
@@ -30,9 +30,9 @@
 
 
 def x_index(num_taps, chans):
-    r, n = grid2(3 * TILE, TILE)
-    index = r // chans - TILE // chans - n // chans + num_taps // 2
-    return valid_index(index, r % chans == n % chans, num_taps)
+    x, n = grid2(3 * TILE // chans, TILE)
+    index = x - TILE // chans - n // chans + num_taps // 2
+    return valid_index(index, n >= 0, num_taps)
 
 
 def y_index(num_taps):
@@ -73,19 +73,30 @@
 
 def band_kernel(taps, wmix, spread, same, xi, yi, zi, xf, xb, yf, yb, zf, zb, wd, wt):
     layers, _, num_taps = taps.shape
-    reps = TILE // spread.shape[0]
-    for axis, index, fwd, bwd in ((0, xi, xf, xb), (1, yi, yf, yb), (2, zi, zf, zb)):
+    chans = spread.shape[0]
+    reps = TILE // chans
+
+    def values(which, axis):
+        zero = jnp.zeros(which.shape, F32)
+        fwd, bwd = [zero] * layers, [zero] * layers
+        for t in range(num_taps):
+            hit = which == t
+            for layer in range(layers):
+                fwd[layer] = jnp.where(hit, taps[layer, axis, t], fwd[layer])
+                bwd[layer] = jnp.where(hit, taps[layer, axis, num_taps - 1 - t], bwd[layer])
+        return fwd, bwd
+
+    diag = lax.rem(lax.broadcasted_iota(jnp.int32, (chans, TILE), 1), chans) == lax.broadcasted_iota(jnp.int32, (chans, TILE), 0)
+    for dst, lines in zip((xf, xb), values(xi[...], 0)):
+        for layer in range(layers):
+            for x in range(xi.shape[0]):
+                line = jnp.broadcast_to(lines[layer][x : x + 1], (chans, TILE))
+                dst[layer, pl.ds(x * chans, chans), :] = jnp.where(diag, line, 0.0).astype(BF16)
+    for axis, index, fwd, bwd in ((1, yi, yf, yb), (2, zi, zf, zb)):
         @pl.loop(0, index.shape[0] // ROWS)
         def _(chunk):
             rows = pl.ds(pl.multiple_of(chunk * ROWS, ROWS), ROWS)
-            which = index[rows, :]
-            zero = jnp.zeros(which.shape, F32)
-            out = [[zero] * layers, [zero] * layers]
-            for t in range(num_taps):
-                hit = which == t
-                for layer in range(layers):
-                    out[0][layer] = jnp.where(hit, taps[layer, axis, t], out[0][layer])
-                    out[1][layer] = jnp.where(hit, taps[layer, axis, num_taps - 1 - t], out[1][layer])
+            out = values(index[rows, :], axis)
             for layer in range(layers):
                 fwd[layer, rows, :] = out[0][layer].astype(BF16)
                 bwd[layer, rows, :] = out[1][layer].astype(BF16)
@@ -104,7 +115,7 @@
     same = jnp.asarray(r // chans == n // chans, jnp.int32)
     indices = [x_index(num_taps, chans), y_index(num_taps), z_index(num_taps, ysub, nz)]
     vmem_spec = pl.BlockSpec(memory_space=pltpu.VMEM)
-    shapes = [i.shape for i in indices for _ in range(2)] + [(TILE, TILE)] * 2
+    shapes = [(3 * TILE, TILE)] * 2 + [i.shape for i in indices[1:] for _ in range(2)] + [(TILE, TILE)] * 2
     return pl.pallas_call(
         band_kernel,
         out_shape=[jax.ShapeDtypeStruct((layers,) + shape, BF16) for shape in shapes],
@@ -114,69 +125,69 @@
     )(filter_taps, w_mix, spread, same, *[jnp.asarray(i) for i in indices])
 
 
-def entry_kernel(src, dst, rows):
-    chans, nx, sub, nz = src.shape
-
-    @pl.loop(0, nx)
-    def _(x):
-        part = src[:, x].astype(F32).reshape(chans * sub, nz)
-        rows[pl.ds(pl.multiple_of(x * chans * sub, chans * sub), chans * sub), :] = part
-
+def relayout(src, dst, rows):
+    chans, nx, ny, nz = src.shape
+    step = ny + SUB
+    for c in range(chans):
+        for x in range(nx):
+            rows[pl.ds((x * chans + c) * step, ny), :] = src[c, x].astype(F32)
     eye = (lax.broadcasted_iota(jnp.int32, (nz, nz), 0) == lax.broadcasted_iota(jnp.int32, (nz, nz), 1)).astype(BF16)
 
-    @pl.loop(0, nx * chans // TILE)
-    def _(tile):
-        for y in range(sub):
-            block = rows[pl.ds(tile * TILE * sub + y, TILE, stride=sub), :].astype(BF16)
+    @pl.loop(0, ny // SUB)
+    def _(part):
+        for i in range(SUB):
+            y = part * SUB + i
+            block = rows[pl.ds(y, TILE, stride=step), :].astype(BF16)
             out = lax.dot_general(eye, block, (((1,), (1,)), ((), ())), preferred_element_type=F32)
-            dst[y, :, lane_ds(tile)] = out.astype(BF16)
+            dst[y] = out.astype(BF16)
 
 
 def to_dense(a):
     chans, nx, ny, nz = a.shape
-    lanes = nx * chans
+    per = TILE // chans
     return pl.pallas_call(
-        entry_kernel,
-        grid=(ny // SUB,),
-        in_specs=[pl.BlockSpec((chans, nx, SUB, nz), lambda i: (0, 0, i, 0))],
-        out_specs=pl.BlockSpec((SUB, nz, lanes), lambda i: (i, 0, 0)),
-        out_shape=jax.ShapeDtypeStruct((ny, nz, lanes), BF16),
-        scratch_shapes=[pltpu.VMEM((lanes * SUB, nz), F32)],
+        relayout,
+        grid=(nx // per,),
+        in_specs=[pl.BlockSpec((chans, per, ny, nz), lambda i: (0, i, 0, 0))],
+        out_specs=pl.BlockSpec((ny, nz, TILE), lambda i: (0, 0, i)),
+        out_shape=jax.ShapeDtypeStruct((ny, nz, nx * chans), BF16),
+        scratch_shapes=[pltpu.VMEM((TILE * (ny + SUB), nz), F32)],
         compiler_params=pltpu.CompilerParams(vmem_limit_bytes=VMEM_BYTES),
         name='to_dense',
     )(a)
 
 
 def leave_kernel(src, dst, rows):
-    sub, nz, lanes = src.shape
+    ny, nz, _ = src.shape
     chans, nx = dst.shape[:2]
+    step = ny + SUB
     eye = (lax.broadcasted_iota(jnp.int32, (TILE, TILE), 0) == lax.broadcasted_iota(jnp.int32, (TILE, TILE), 1)).astype(BF16)
     pad = jnp.zeros((LANE - nz, TILE), BF16)
 
-    @pl.loop(0, lanes // TILE)
-    def _(tile):
-        for y in range(0, sub, 2):
-            block = jnp.concatenate([src[y, :, lane_ds(tile)], pad, src[y + 1, :, lane_ds(tile)], pad], axis=0)
+    @pl.loop(0, ny // SUB)
+    def _(part):
+        for i in range(0, SUB, 2):
+            y = part * SUB + i
+            block = jnp.concatenate([src[y], pad, src[y + 1], pad], axis=0)
             out = lax.dot_general(eye, block, (((1,), (1,)), ((), ())), preferred_element_type=F32)
-            rows[pl.ds(tile * TILE * sub + y, TILE, stride=sub), :] = out[:, :LANE]
-            rows[pl.ds(tile * TILE * sub + y + 1, TILE, stride=sub), :] = out[:, LANE:]
-
-    @pl.loop(0, nx)
-    def _(x):
-        part = rows[pl.ds(pl.multiple_of(x * chans * sub, chans * sub), chans * sub), :]
-        dst[:, x] = part[:, :nz].astype(BF16).reshape(chans, sub, nz)
+            rows[pl.ds(y, TILE, stride=step), :] = out[:, :LANE]
+            rows[pl.ds(y + 1, TILE, stride=step), :] = out[:, LANE:]
+
+    for c in range(chans):
+        for x in range(nx):
+            dst[c, x] = rows[pl.ds((x * chans + c) * step, ny), :][:, :nz].astype(BF16)
 
 
 def from_dense(a, chans):
     ny, nz, lanes = a.shape
-    nx = lanes // chans
+    per = TILE // chans
     return pl.pallas_call(
         leave_kernel,
-        grid=(ny // SUB,),
-        in_specs=[pl.BlockSpec((SUB, nz, lanes), lambda i: (i, 0, 0))],
-        out_specs=pl.BlockSpec((chans, nx, SUB, nz), lambda i: (0, 0, i, 0)),
-        out_shape=jax.ShapeDtypeStruct((chans, nx, ny, nz), BF16),
-        scratch_shapes=[pltpu.VMEM((lanes * SUB, LANE), F32)],
+        grid=(lanes // TILE,),
+        in_specs=[pl.BlockSpec((ny, nz, TILE), lambda i: (0, 0, i))],
+        out_specs=pl.BlockSpec((chans, per, ny, nz), lambda i: (0, i, 0, 0)),
+        out_shape=jax.ShapeDtypeStruct((chans, lanes // chans, ny, nz), BF16),
+        scratch_shapes=[pltpu.VMEM((TILE * (ny + SUB), LANE), F32)],
         compiler_params=pltpu.CompilerParams(vmem_limit_bytes=VMEM_BYTES),
         name='from_dense',
     )(a)
@@ -322,7 +333,7 @@
         emit(g, dot(lhs, rhs).astype(BF16).reshape(ysub, nz, TILE))
 
 
-def fwd_kernel(half, sizes, v_hbm, wx, ly, lz, wd, bias, a3_hbm, vol, xh, a1, yr, a2, zs, zr, a3, in_sem, out_sem, xsend, xrecv, ysend, yrecv, zsend, zrecv):
+def fwd_kernel(half, sizes, v_hbm, cot_hbm, wx, ly, lz, wd, bias, a3_hbm, g_hbm, cbuf, crow, gbuf, cin_sem, gout_sem, vol, xh, a1, yr, a2, zs, zr, a3, in_sem, out_sem, xsend, xrecv, ysend, yrecv, zsend, zrecv):
     ny, nz, lanes, tiles, group, ysub = dims(v_hbm.shape, half)
     layers = wx.shape[0]
     links = Links(sizes)
@@ -351,10 +362,22 @@
     def x_at(slot):
         return links.x_edge(vol, xh, xsems, slot, lanes)
 
+    chans = cot_hbm.shape[0]
+    per, sub = TILE // chans, ny // layers
+
+    def cot_in(item):
+        j, q = item // layers, lax.rem(item, layers)
+        return pltpu.make_async_copy(cot_hbm.at[:, pl.ds(j * per, per), pl.ds(pl.multiple_of(q * sub, SUB), sub), :], cbuf.at[lax.rem(item, 2)], cin_sem.at[lax.rem(item, 2)])
+
+    def cot_out(item):
+        j, q = item // layers, lax.rem(item, layers)
+        return pltpu.make_async_copy(gbuf.at[lax.rem(item, 2)], g_hbm.at[pl.ds(q * sub, sub), :, lane_ds(j)], gout_sem.at[lax.rem(item, 2)])
+
     edge_tile = place(tiles - 1)[2]
     fetch(edge_tile).start()
     for p in range(tiles - 1):
         fetch(place(p)[2]).start()
+    cot_in(0).start()
     links.zero_edges('gy', yr)
     links.zero_edges('gz', zr)
     links.barrier()
@@ -446,6 +469,18 @@
                 pl.when(p == tiles - 1)(x_at(1 - slot).start)
 
             put(layer, tile).start()
+
+        @pl.when(step < total)
+        def _():
+            slot = lax.rem(step, 2)
+            cot_in(step).wait()
+            pl.when(step + 1 < total)(cot_in(step + 1).start)
+            pl.when(step >= 2)(cot_out(step - 2).wait)
+            relayout(cbuf.at[slot], gbuf.at[slot], crow)
+            cot_out(step).start()
+
+    cot_out(total - 2).wait()
+    cot_out(total - 1).wait()
 
     @pl.loop(0, tiles)
     def _(tile):
@@ -682,15 +717,18 @@
         z_send = pltpu.VMEM((2, ny // ysub, ROWS, lanes), BF16)
         z_halo = pltpu.VMEM((2, 2, ny // ysub, ROWS, lanes), BF16)
 
-        acts = pl.pallas_call(
+        per, sub = TILE // chans, ny // layers
+        acts, cot = pl.pallas_call(
             functools.partial(fwd_kernel, half, sizes),
-            out_shape=jax.ShapeDtypeStruct((layers, ny, nz, lanes), BF16),
-            in_specs=[any_spec] + [vmem_spec] * 5,
-            out_specs=any_spec,
-            scratch_shapes=[full, two, full, y_halo, full, z_send, z_halo, full, dma((tiles,)), dma((tiles,))] + link_sems(tiles),
+            out_shape=[jax.ShapeDtypeStruct((layers, ny, nz, lanes), BF16), jax.ShapeDtypeStruct((ny, nz, lanes), BF16)],
+            in_specs=[any_spec] * 2 + [vmem_spec] * 5,
+            out_specs=[any_spec] * 2,
+            scratch_shapes=[pltpu.VMEM((2, chans, per, sub, nz), BF16), pltpu.VMEM((TILE * (sub + SUB), nz), F32), pltpu.VMEM((2, sub, nz, TILE), BF16), dma((2,)), dma((2,))]
+            + [full, two, full, y_halo, full, z_send, z_halo, full, dma((tiles,)), dma((tiles,))]
+            + link_sems(tiles),
             compiler_params=params(collective_id=0),
             name='fwd_layers',
-        )(to_dense(volume), wx_f, ly_f, lz_f, wd, bias)
+        )(to_dense(volume), cot_out, wx_f, ly_f, lz_f, wd, bias)
         rounds = sum((size - 1).bit_length() for size in sizes.values())
         sum_shape = (layers, chans + 8, TILE)
         grad, sums = pl.pallas_call(
@@ -704,7 +742,7 @@
             + link_sems(tiles),
             compiler_params=params(collective_id=1),
             name='bwd_layers',
-        )(acts, to_dense(cot_out), wx_b, ly_b, lz_b, pick, wd, wt, bias)
+        )(acts, cot, wx_b, ly_b, lz_b, pick, wd, wt, bias)
         blocks = sums.reshape(layers, chans + 8, reps, chans).sum(axis=2)
         return from_dense(grad, chans), blocks[:, :chans], blocks[:, chans:].sum(axis=1)
 

time: 251 us -> 230 us (0.916)
  Pallas kernels: 246 us -> 224 us
    pallas_call x4 -> x3, Pallas kernels: 130 us -> 112 us  [the longest x1 76.7 us: local_step(): pl.pallas_call(functools.partial(fwd_kernel, half, sizes), out_shape=[jax...]
    pallas_call x1, Pallas kernels: 8.24 us -> 4.79 us  [band_weights(): pl.pallas_call(band_kernel, out_shape=[jax.ShapeDtypeStruct((layers,) + s...]
where the time goes in v5:
time: 230 us; the launch traced here: 229 us
  Pallas kernels  224 us (97%)
  local copies, waits for them, and re-layouts  3.03 us (1%)
    pallas_call x1, Pallas kernels, local_step(): pl.pallas_call(functools.partial(bwd_kernel, half, sizes, chans), out_sha...  108 us
    pallas_call x1, Pallas kernels, local_step(): pl.pallas_call(functools.partial(fwd_kernel, half, sizes), out_shape=[jax...  76.7 us
    pallas_call x1, Pallas kernels, from_dense(): pl.pallas_call(leave_kernel, grid=(lanes // TILE,), in_specs=[pl.BlockSpe...  18 us
    pallas_call x1, Pallas kernels, to_dense(): pl.pallas_call(relayout, grid=(nx // per,), in_specs=[pl.BlockSpec((chans...  16.9 us
    pallas_call x1, Pallas kernels, band_weights(): pl.pallas_call(band_kernel, out_shape=[jax.ShapeDtypeStruct((layers,) + s...  4.79 us

profile of v5, /device:TPU:97, one launch (start us, length us, event | category | flops | bytes accessed | tf_op | source)
XLA Modules:
  0.0 228.6 jit_solution(16266440701891108514)
XLA Ops:
  0.6 0.7 tile.8
  1.3 0.7 tile.9.bias
  2.0 4.8 %band_weights.1 = (bf16[3,768,256]{2,1,0:T(8,128)(2,1)}, bf16[3,768,256]{2,1,0:T(8,128)(2,1)}, bf16[3,160,256]{2,1,0:T(8,128)(2,1)}, bf16[3,160,256]{2,1,0:T(8,1...) custom-call(f32[3,3,11]{2,1,0:T(4,128)} %taps.1, ...), custom_call_target="tpu_custom_call" | custom-call | tf_op jit(solution)/shard_map/band_weights/pallas_call | solution.py:119
  6.8 16.9 %to_dense.1.v_hbm = bf16[48,48,1536]{2,1,0:T(8,128)(2,1)} custom-call(bf16[32,48,48,48]{3,2,1,0:T(8,128)(2,1)} %src.1), custom_call_target="tpu_custom_call" | custom-call | tf_op jit(solution)/shard_map/to_dense/pallas_call | solution.py:148
  23.7 76.7 %fwd_layers.1 = (bf16[3,48,48,1536]{3,2,1,0:T(8,128)(2,1)}, bf16[48,48,1536]{2,1,0:T(8,128)(2,1)}) custom-call(bf16[48,48,1536]{2,1,0:T(8,128)(2,1)} %to_dense.1.v_hbm, bf16[32,48,48,48]{3,2,1,0:T(8,128)(2,1)} %cot_hbm.1, bf16[3,768,256]{2,1,0:T(8,128)(2,1)} %get-tuple-element.15.wx, bf16[3,160,256]{2,1,0:T(8,128)(2,1)} %get-tuple-element.16.ly, ...), custom_call_target="tpu_custom_call" | custom-call | tf_op jit(solution)/shard_map/fwd_layers/pallas_call | solution.py:721
  100.4 107.7 %bwd_layers.1 = (bf16[48,48,1536]{2,1,0:T(8,128)(2,1)}, f32[3,40,256]{2,1,0:T(8,128)}) custom-call(bf16[3,48,48,1536]{3,2,1,0:T(8,128)(2,1)} %get-tuple-element.19.a3_hbm, bf16[48,48,1536]{2,1,0:T(8,128)(2,1)} %get-tuple-element.20.g_hbm, bf16[3,768,256]{2,1,0:T(8,128)(2,1)} %get-tuple-element.21.wx, bf16[3,160,256]{2,1,0:T(8,128)(2,1)} %get-tuple-element.22.ly, ...), custom_call_target="tpu_custom_call" | custom-call | tf_op jit(solution)/shard_map/bwd_layers/pallas_call | solution.py:734
  208.2 1.1 reshape.15
  209.2 0.1 reduce_sum.18
  209.4 0.6 slice_reduce_fusion
  210.0 0.6 slice.8
  210.6 18.0 %from_dense.1 = bf16[32,48,48,48]{3,2,1,0:T(8,128)(2,1)} custom-call(bf16[48,48,1536]{2,1,0:T(8,128)(2,1)} %get-tuple-element.25.src), custom_call_target="tpu_custom_call" | custom-call | tf_op jit(solution)/shard_map/from_dense/pallas_call | solution.py:184

commit v6 on v5

--- a/solution.py
+++ b/solution.py
@@ -71,7 +71,7 @@
     return jnp.asarray(hit, BF16)
 
 
-def band_kernel(taps, wmix, spread, same, xi, yi, zi, xf, xb, yf, yb, zf, zb, wd, wt):
+def band_kernel(taps, wmix, bmix, spread, same, xi, yi, zi, xf, xb, yf, yb, zf, zb, wd, wt, bias):
     layers, _, num_taps = taps.shape
     chans = spread.shape[0]
     reps = TILE // chans
@@ -101,13 +101,14 @@
                 fwd[layer, rows, :] = out[0][layer].astype(BF16)
                 bwd[layer, rows, :] = out[1][layer].astype(BF16)
     for layer in range(layers):
+        bias[layer] = jnp.concatenate([bmix[pl.ds(layer, 1), :]] * reps, axis=1)
         for dst, axis in ((wd, 1), (wt, 0)):
             wide = lax.dot_general(wmix[layer], spread[...], (((axis,), (0,)), ((), ())), preferred_element_type=F32)
             full = jnp.concatenate([wide] * reps, axis=0)
             dst[layer] = jnp.where(same[...] != 0, full, 0.0).astype(BF16)
 
 
-def band_weights(filter_taps, w_mix, ysub, nz):
+def band_weights(filter_taps, w_mix, b_mix, ysub, nz):
     layers, _, num_taps = filter_taps.shape
     chans = w_mix.shape[1]
     r, n = grid2(TILE, TILE)
@@ -118,16 +119,16 @@
     shapes = [(3 * TILE, TILE)] * 2 + [i.shape for i in indices[1:] for _ in range(2)] + [(TILE, TILE)] * 2
     return pl.pallas_call(
         band_kernel,
-        out_shape=[jax.ShapeDtypeStruct((layers,) + shape, BF16) for shape in shapes],
-        in_specs=[pl.BlockSpec(memory_space=pltpu.SMEM)] + [vmem_spec] * 6,
-        out_specs=[vmem_spec] * 8,
+        out_shape=[jax.ShapeDtypeStruct((layers,) + shape, BF16) for shape in shapes] + [jax.ShapeDtypeStruct((layers, 1, TILE), F32)],
+        in_specs=[pl.BlockSpec(memory_space=pltpu.SMEM)] + [vmem_spec] * 7,
+        out_specs=[vmem_spec] * 9,
         name='band_weights',
-    )(filter_taps, w_mix, spread, same, *[jnp.asarray(i) for i in indices])
+    )(filter_taps, w_mix, b_mix, spread, same, *[jnp.asarray(i) for i in indices])
 
 
 def relayout(src, dst, rows):
     chans, nx, ny, nz = src.shape
-    step = ny + SUB
+    step = ny + 1
     for c in range(chans):
         for x in range(nx):
             rows[pl.ds((x * chans + c) * step, ny), :] = src[c, x].astype(F32)
@@ -151,7 +152,7 @@
         in_specs=[pl.BlockSpec((chans, per, ny, nz), lambda i: (0, i, 0, 0))],
         out_specs=pl.BlockSpec((ny, nz, TILE), lambda i: (0, 0, i)),
         out_shape=jax.ShapeDtypeStruct((ny, nz, nx * chans), BF16),
-        scratch_shapes=[pltpu.VMEM((TILE * (ny + SUB), nz), F32)],
+        scratch_shapes=[pltpu.VMEM((TILE * (ny + 1), nz), F32)],
         compiler_params=pltpu.CompilerParams(vmem_limit_bytes=VMEM_BYTES),
         name='to_dense',
     )(a)
@@ -160,7 +161,7 @@
 def leave_kernel(src, dst, rows):
     ny, nz, _ = src.shape
     chans, nx = dst.shape[:2]
-    step = ny + SUB
+    step = ny + 1
     eye = (lax.broadcasted_iota(jnp.int32, (TILE, TILE), 0) == lax.broadcasted_iota(jnp.int32, (TILE, TILE), 1)).astype(BF16)
     pad = jnp.zeros((LANE - nz, TILE), BF16)
 
@@ -187,7 +188,7 @@
         in_specs=[pl.BlockSpec((ny, nz, TILE), lambda i: (0, 0, i))],
         out_specs=pl.BlockSpec((chans, per, ny, nz), lambda i: (0, i, 0, 0)),
         out_shape=jax.ShapeDtypeStruct((chans, lanes // chans, ny, nz), BF16),
-        scratch_shapes=[pltpu.VMEM((TILE * (ny + SUB), LANE), F32)],
+        scratch_shapes=[pltpu.VMEM((TILE * (ny + 1), LANE), F32)],
         compiler_params=pltpu.CompilerParams(vmem_limit_bytes=VMEM_BYTES),
         name='from_dense',
     )(a)
@@ -706,9 +707,8 @@
         reps = TILE // chans
         ysub = (ROWS - 2 * half) // 2
         params = functools.partial(pltpu.CompilerParams, has_side_effects=True, vmem_limit_bytes=VMEM_BYTES)
-        wx_f, wx_b, ly_f, ly_b, lz_f, lz_b, wd, wt = band_weights(filter_taps, w_mix, ysub, nz)
+        wx_f, wx_b, ly_f, ly_b, lz_f, lz_b, wd, wt, bias = band_weights(filter_taps, w_mix, b_mix, ysub, nz)
         pick = pick_matrix(half, ysub, nz)
-        bias = jnp.tile(b_mix, (1, reps))[:, None, :]
 
         full = pltpu.VMEM((ny, nz, lanes), BF16)
         one = (ny, nz, TILE)
@@ -723,7 +723,7 @@
             out_shape=[jax.ShapeDtypeStruct((layers, ny, nz, lanes), BF16), jax.ShapeDtypeStruct((ny, nz, lanes), BF16)],
             in_specs=[any_spec] * 2 + [vmem_spec] * 5,
             out_specs=[any_spec] * 2,
-            scratch_shapes=[pltpu.VMEM((2, chans, per, sub, nz), BF16), pltpu.VMEM((TILE * (sub + SUB), nz), F32), pltpu.VMEM((2, sub, nz, TILE), BF16), dma((2,)), dma((2,))]
+            scratch_shapes=[pltpu.VMEM((2, chans, per, sub, nz), BF16), pltpu.VMEM((TILE * (sub + 1), nz), F32), pltpu.VMEM((2, sub, nz, TILE), BF16), dma((2,)), dma((2,))]
             + [full, two, full, y_halo, full, z_send, z_halo, full, dma((tiles,)), dma((tiles,))]
             + link_sems(tiles),
             compiler_params=params(collective_id=0),

time: 230 us -> 226 us (0.983)
  Pallas kernels: 224 us -> 221 us
where the time goes in v6:
time: 226 us; the launch traced here: 225 us
  Pallas kernels  221 us (98%)
    pallas_call x1, Pallas kernels, local_step(): pl.pallas_call(functools.partial(bwd_kernel, half, sizes, chans), out_sha...  107 us
    pallas_call x1, Pallas kernels, local_step(): pl.pallas_call(functools.partial(fwd_kernel, half, sizes), out_shape=[jax...  76.2 us
    pallas_call x1, Pallas kernels, from_dense(): pl.pallas_call(leave_kernel, grid=(lanes // TILE,), in_specs=[pl.BlockSpe...  16.8 us
    pallas_call x1, Pallas kernels, to_dense(): pl.pallas_call(relayout, grid=(nx // per,), in_specs=[pl.BlockSpec((chans...  16.4 us
    pallas_call x1, Pallas kernels, band_weights(): pl.pallas_call(band_kernel, out_shape=[jax.ShapeDtypeStruct((layers,) + s...  4.84 us

profile of v6, /device:TPU:97, one launch (start us, length us, event | category | flops | bytes accessed | tf_op | source)
XLA Modules:
  0.0 224.6 jit_solution(14809072630886749954)
XLA Ops:
  0.6 4.8 %band_weights.1 = (bf16[3,768,256]{2,1,0:T(8,128)(2,1)}, bf16[3,768,256]{2,1,0:T(8,128)(2,1)}, bf16[3,160,256]{2,1,0:T(8,128)(2,1)}, bf16[3,160,256]{2,1,0:T(8,1...) custom-call(f32[3,3,11]{2,1,0:T(4,128)} %taps.1, ...), custom_call_target="tpu_custom_call" | custom-call | tf_op jit(solution)/shard_map/band_weights/pallas_call | solution.py:120
  5.5 16.4 %to_dense.1.v_hbm = bf16[48,48,1536]{2,1,0:T(8,128)(2,1)} custom-call(bf16[32,48,48,48]{3,2,1,0:T(8,128)(2,1)} %src.1), custom_call_target="tpu_custom_call" | custom-call | tf_op jit(solution)/shard_map/to_dense/pallas_call | solution.py:149
  21.8 76.2 %fwd_layers.1 = (bf16[3,48,48,1536]{3,2,1,0:T(8,128)(2,1)}, bf16[48,48,1536]{2,1,0:T(8,128)(2,1)}) custom-call(bf16[48,48,1536]{2,1,0:T(8,128)(2,1)} %to_dense.1.v_hbm, bf16[32,48,48,48]{3,2,1,0:T(8,128)(2,1)} %cot_hbm.1, bf16[3,768,256]{2,1,0:T(8,128)(2,1)} %get-tuple-element.16.wx, bf16[3,160,256]{2,1,0:T(8,128)(2,1)} %get-tuple-element.17.ly, ...), custom_call_target="tpu_custom_call" | custom-call | tf_op jit(solution)/shard_map/fwd_layers/pallas_call | solution.py:721
  98.1 107.3 %bwd_layers.1 = (bf16[48,48,1536]{2,1,0:T(8,128)(2,1)}, f32[3,40,256]{2,1,0:T(8,128)}) custom-call(bf16[3,48,48,1536]{3,2,1,0:T(8,128)(2,1)} %get-tuple-element.21.a3_hbm, bf16[48,48,1536]{2,1,0:T(8,128)(2,1)} %get-tuple-element.22.g_hbm, bf16[3,768,256]{2,1,0:T(8,128)(2,1)} %get-tuple-element.23.wx, bf16[3,160,256]{2,1,0:T(8,128)(2,1)} %get-tuple-element.24.ly, ...), custom_call_target="tpu_custom_call" | custom-call | tf_op jit(solution)/shard_map/bwd_layers/pallas_call | solution.py:734
  205.3 1.1 reshape.9
  206.4 0.1 reduce_sum.18
  206.6 0.6 slice_reduce_fusion
  207.2 0.6 slice.8
  207.8 16.8 %from_dense.1 = bf16[32,48,48,48]{3,2,1,0:T(8,128)(2,1)} custom-call(bf16[48,48,1536]{2,1,0:T(8,128)(2,1)} %get-tuple-element.27.src), custom_call_target="tpu_custom_call" | custom-call | tf_op jit(solution)/shard_map/from_dense/pallas_call | solution.py:185
